TPU v7x, 16 devices: a 4x2x1 block of a 4x4x8 slice. The times are simulated.
16 devices in a mesh: rep: 2 (over y, z), dp: 8 (over x, core).
Axes of the slice: x: 4, y: 2, z: 1, core: 2. Of those that a mesh axis runs over, the one named last changes fastest.
The devices are a block of a 4x4x8 slice.
Arguments:
- x: bfloat16 [16, 2048, 1024], P(('rep', 'dp')), parts along dimension 0
- dy: bfloat16 [16, 2048, 1024], P(('rep', 'dp')), parts along dimension 0
- w_gate: bfloat16 [2, 1024, 3200], replicated
- w_up: bfloat16 [2, 1024, 3200], replicated
- w_down: bfloat16 [2, 3200, 1024], replicated
- m_w_gate: float32 [2, 1024, 3200], P(None, 'dp')
- m_w_up: float32 [2, 1024, 3200], P(None, 'dp')
- m_w_down: float32 [2, 3200, 1024], P(None, 'dp')
- v_w_gate: float32 [2, 1024, 3200], P(None, 'dp')
- v_w_up: float32 [2, 1024, 3200], P(None, 'dp')
- v_w_down: float32 [2, 3200, 1024], P(None, 'dp')
Outputs:
- output 1: bfloat16 [4, 1024, 3200], P('rep'), parts along dimension 0
- output 2: bfloat16 [4, 1024, 3200], P('rep'), parts along dimension 0
- output 3: bfloat16 [4, 3200, 1024], P('rep'), parts along dimension 0
- output 4: float32 [4, 1024, 3200], P('rep', 'dp'), parts along dimension 0
- output 5: float32 [4, 1024, 3200], P('rep', 'dp'), parts along dimension 0
- output 6: float32 [4, 3200, 1024], P('rep', 'dp'), parts along dimension 0
- output 7: float32 [4, 1024, 3200], P('rep', 'dp'), parts along dimension 0
- output 8: float32 [4, 1024, 3200], P('rep', 'dp'), parts along dimension 0
- output 9: float32 [4, 3200, 1024], P('rep', 'dp'), parts along dimension 0
There are 2 independent parts. A program takes and returns all parts, laid end to end along the dimension named above; an argument that names none is the same for every part.
All inputs are finite; a program needn't handle non-finite values.
Results may differ from a plain program's by a relative error of at most 0.022.
Values are sent between devices in bfloat16 or wider.
A program may use at most 768 MiB of HBM per device.

v0:
```python
import jax
import jax.numpy as jnp
from jax import lax

NAMES = ("w_gate", "w_up", "w_down")


def matmul(a, w):
    return jnp.dot(a, w, preferred_element_type=jnp.float32).astype(jnp.bfloat16)


def normed(h):
    wide = h.astype(jnp.float32)
    scale = lax.rsqrt(jnp.mean(wide**2, -1, keepdims=True) + 1e-6)
    return (wide * scale).astype(jnp.bfloat16)


def layer(h, w):
    a = normed(h)
    gate = jnp.dot(a, w["w_gate"], preferred_element_type=jnp.float32)
    up = jnp.dot(a, w["w_up"], preferred_element_type=jnp.float32)
    return h + matmul((jax.nn.silu(gate) * up).astype(jnp.bfloat16), w["w_down"])


def adamw(w, m, v, g):
    m = 0.9 * m + 0.1 * g
    v = 0.95 * v + 0.05 * g * g
    step = m * lax.rsqrt(v + 1e-8) + 0.1 * w
    return (w - 0.02 * step).astype(jnp.bfloat16), m, v


def stack(weights, h):
    for number in range(weights["w_gate"].shape[0]):
        h = layer(h, {name: w[number] for name, w in weights.items()})
    return h


def solution(mesh):
    groups = mesh.shape["rep"]

    def step(x, dy, *arrays):
        weights, m, v = (arrays[i : i + 3] for i in (0, 3, 6))
        x, dy = (t.reshape(groups, -1, *t.shape[1:]) for t in (x, dy))

        def of_a_group(x, dy):
            _, back = jax.vjp(lambda w: stack(w, x), dict(zip(NAMES, weights, strict=True)))
            by_weights = back(dy)[0]
            gradients = [by_weights[name].astype(jnp.float32) for name in NAMES]
            new = [adamw(w.astype(jnp.float32), m, v, g) for w, m, v, g in zip(weights, m, v, gradients, strict=True)]
            return tuple(one[which] for which in range(3) for one in new)

        return tuple(t.reshape(-1, *t.shape[2:]) for t in jax.vmap(of_a_group)(x, dy))

    return step
```

profile of v0, /device:TPU:113, one launch (start us, length us, event | category | flops | bytes accessed | tf_op | source)
XLA Modules:
  0.0 905.7 jit_solution(13868921095941854295)
XLA Ops:
  10.3 6.6 copy
  17.0 22.0 %fusion.67 = f32[2048,3200]{1,0:T(8,128)} fusion(bf16[2,1024,3200]{2,1,0:T(8,128)(2,1)} %param, bf16[1,2048,1024]{2,1,0:T(8,128)(2,1)} %param.2, f32[2048]{0:T(1024)S(1)} %add_rsqrt_fusion), kind=kOutput, calls=%fused_computation.79 | convolution fusion | flops 13428064256 | bytes 36970496 | tf_op jit(solution)/vmap(jvp())/dot_general | solution.py:20
  39.0 18.1 %fusion.65 = f32[2048,3200]{1,0:T(8,128)} fusion(bf16[2,1024,3200]{2,1,0:T(8,128)(2,1)S(1)} %bitcast.335, bf16[1,2048,1024]{2,1,0:T(8,128)(2,1)S(1)} %copy-done.1, f32[2048]{0:T(1024)S(1)} %add_rsqrt_fusion), kind=kOutput, calls=%fused_computation.77 | convolution fusion | flops 13428064256 | bytes 36970496 | tf_op jit(solution)/vmap(jvp())/dot_general | solution.py:21
  57.1 22.9 %fusion.26 = bf16[2048,3200]{1,0:T(8,128)(2,1)} fusion(f32[2048,3200]{1,0:T(8,128)} %fusion.65, f32[2048,3200]{1,0:T(8,128)} %fusion.67), kind=kLoop, calls=%fused_computation.41 | loop fusion | flops 39321600 | bytes 65536000
  80.0 22.1 %fusion.51 = (f32[2048]{0:T(1024)S(1)}, bf16[1,1,2048,1024]{2,3,1,0:T(8,128)(2,1)}) fusion(bf16[2048,3200]{1,0:T(8,128)(2,1)} %fusion.26, bf16[2,3200,1024]{2,1,0:T(8,128)(2,1)} %param.4, bf16[1,2048,1024]{1,2,0:T(8,128)(2,1)} %copy), kind=kOutput, calls=%fused_computation.62 | convolution fusion | flops 13432256512 | bytes 28057600 | tf_op jit(solution)/vmap(jvp())/dot_general | solution.py:9
  102.7 23.4 %fusion.54 = f32[2048,3200]{1,0:T(8,128)} fusion(bf16[2,1024,3200]{2,1,0:T(8,128)(2,1)} %param, bf16[1,1,2048,1024]{2,3,1,0:T(8,128)(2,1)} %get-tuple-element.10, f32[2048]{0:T(1024)S(1)} %bitcast.339), kind=kOutput, calls=%fused_computation.66 | convolution fusion | flops 13428064256 | bytes 36970496 | tf_op jit(solution)/vmap(jvp())/dot_general | solution.py:20
  126.1 20.8 %fusion.58 = f32[2048,3200]{1,0:T(8,128)} fusion(bf16[2,1024,3200]{2,1,0:T(8,128)(2,1)} %param.3, bf16[1,1,2048,1024]{2,3,1,0:T(8,128)(2,1)S(1)} %copy-done.3, f32[2048]{0:T(1024)S(1)} %bitcast.340), kind=kOutput, calls=%fused_computation.70 | convolution fusion | flops 13428064256 | bytes 36970496 | tf_op jit(solution)/vmap(jvp())/dot_general | solution.py:21
  146.9 28.5 %fusion.35 = f32[1,3200,1024]{2,1,0:T(8,128)} fusion(f32[2048,3200]{1,0:T(8,128)} %fusion.58, f32[2048,3200]{1,0:T(8,128)} %fusion.54, bf16[1,2048,1024]{2,1,0:T(8,128)(2,1)} %param.5), kind=kOutput, calls=%fused_computation.52 | convolution fusion | flops 13461094400 | bytes 69730304 | tf_op jit(solution)/vmap(transpose(jvp()))/dot_general | solution.py:9
  175.5 6.5 copy.1
  182.0 20.8 %convolution_convert_fusion.1 = bf16[2048,3200]{1,0:T(8,128)(2,1)} fusion(bf16[2,3200,1024]{2,1,0:T(8,128)(2,1)} %param.4, bf16[1,2048,1024]{2,1,0:T(8,128)(2,1)} %param.5), kind=kOutput, calls=%fused_computation.36 | convolution fusion | flops 13428326400 | bytes 23855104 | tf_op jit(solution)/vmap(transpose(jvp()))/dot_general | solution.py:9
  202.8 26.9 %fusion.6 = bf16[2048,3200]{1,0:T(8,128)(2,1)} fusion(f32[2048,3200]{1,0:T(8,128)} %fusion.54, f32[2048,3200]{1,0:T(8,128)} %fusion.58, bf16[2048,3200]{1,0:T(8,128)(2,1)} %convolution_convert_fusion.1), kind=kLoop, calls=%fused_computation.11 | loop fusion | flops 78643200 | bytes 78643200
  229.7 22.5 %fusion.24 = bf16[2048,1024]{0,1:T(8,128)(2,1)} fusion(bf16[2048,3200]{1,0:T(8,128)(2,1)} %convolution_convert_fusion.1, f32[2048,3200]{1,0:T(8,128)} %fusion.54, bf16[2,1024,3200]{2,1,0:T(8,128)(2,1)} %param.3), kind=kOutput, calls=%fused_computation.34 | convolution fusion | flops 13461094400 | bytes 50069504 | tf_op jit(solution)/vmap(transpose(jvp()))/dot_general | solution.py:21
  252.2 23.3 %fusion.53 = (f32[2048]{0:T(1024)S(1)}, bf16[2048,1024]{0,1:T(8,128)(2,1)}) fusion(bf16[1,1,2048,1024]{2,3,1,0:T(8,128)(2,1)} %get-tuple-element.10, bf16[2048,1024]{0,1:T(8,128)(2,1)} %fusion.24, bf16[2048,3200]{1,0:T(8,128)(2,1)} %fusion.6, bf16[2,1024,3200]{2,1,0:T(8,128)(2,1)} %param), kind=kOutput, calls=%fused_computation.64 | convolution fusion | flops 13432256512 | bytes 32251904 | tf_op jit(solution)/vmap(transpose(jvp()))/dot_general | solution.py:20
  275.6 5.3 fusion.81
  282.9 19.7 %convolution_bitcast_fusion.1 = f32[1,3200,1024]{2,1,0:T(8,128)} fusion(bf16[2048,3200]{1,0:T(8,128)(2,1)} %fusion.26, bf16[2048,1024]{0,1:T(8,128)(2,1)S(1)} %fusion.81), kind=kOutput, calls=%fused_computation.57 | convolution fusion | flops 13421772800 | bytes 30408704 | tf_op jit(solution)/vmap(transpose(jvp()))/dot_general | solution.py:9
  302.7 22.0 %convolution_bitcast_fusion = f32[1,1024,3200]{2,1,0:T(8,128)} fusion(bf16[2048,3200]{1,0:T(8,128)(2,1)} %fusion.6, bf16[1,1,2048,1024]{2,3,1,0:T(8,128)(2,1)} %get-tuple-element.10, f32[2048]{0:T(1024)S(1)} %bitcast.342), kind=kOutput, calls=%fused_computation.55 | convolution fusion | flops 13428064256 | bytes 30416896 | tf_op jit(solution)/vmap(transpose(jvp()))/dot_general | solution.py:20
  324.9 21.2 %convolution_convert_fusion = bf16[2048,3200]{1,0:T(8,128)(2,1)} fusion(bf16[2048,1024]{0,1:T(8,128)(2,1)} %copy-done.4, bf16[2,3200,1024]{2,1,0:T(8,128)(2,1)} %param.4), kind=kOutput, calls=%fused_computation.35 | convolution fusion | flops 13428326400 | bytes 23855104 | tf_op jit(solution)/vmap(transpose(jvp()))/dot_general | solution.py:9
  346.1 31.9 %fusion.44 = f32[1,1024,3200]{2,1,0:T(8,128)} fusion(f32[2048,3200]{1,0:T(8,128)} %fusion.67, f32[2048,3200]{1,0:T(8,128)} %fusion.65, bf16[2048,3200]{1,0:T(8,128)(2,1)} %convolution_convert_fusion, bf16[1,2048,1024]{1,2,0:T(8,128)(2,1)S(1)} %copy-done.5, f32[2048]{0:T(1024)S(1)} %copy-done.14), kind=kOutput, calls=%fused_computation.56 | convolution fusion | flops 13500153856 | bytes 82845696 | tf_op jit(solution)/vmap(transpose(jvp()))/dot_general | solution.py:20
  378.2 26.1 %fusion.38 = f32[1,1024,3200]{2,1,0:T(8,128)} fusion(bf16[2048,3200]{1,0:T(8,128)(2,1)} %convolution_convert_fusion.1, f32[2048,3200]{1,0:T(8,128)} %fusion.54, bf16[1,1,2048,1024]{2,3,1,0:T(8,128)(2,1)} %get-tuple-element.10, f32[2048]{0:T(1024)S(1)} %bitcast.343), kind=kOutput, calls=%fused_computation.53 | convolution fusion | flops 13467385856 | bytes 56631296 | tf_op jit(solution)/vmap(transpose(jvp()))/dot_general | solution.py:21
  404.4 25.8 %fusion.41 = f32[1,1024,3200]{2,1,0:T(8,128)} fusion(bf16[2048,3200]{1,0:T(8,128)(2,1)} %convolution_convert_fusion, f32[2048,3200]{1,0:T(8,128)} %fusion.67, bf16[1,2048,1024]{1,2,0:T(8,128)(2,1)} %copy, f32[2048]{0:T(1024)S(1)} %copy-done.14), kind=kOutput, calls=%fused_computation.54 | convolution fusion | flops 13467385856 | bytes 56631296 | tf_op jit(solution)/vmap(transpose(jvp()))/dot_general | solution.py:21
  436.1 6.2 fusion.121
  442.5 6.5 reduce-scatter.19.cloned.1.call-done
  451.4 70.9 %reduce-scatter.21.cloned.1.call-done = f32[1,128,3200]{2,1,0:T(8,128)} async-done(((f32[1,1024,3200]{2,1,0:T(8,128)}), f32[1,128,3200]{2,1,0:T(8,128)}) %reduce-scatter.21.cloned.1.call-update) | async-done | bytes 1638416
  523.8 6.0 fusion.123
  529.9 65.1 %reduce-scatter.23.cloned.1.call-done = f32[1,128,3200]{2,1,0:T(8,128)} async-done(((f32[1,1024,3200]{2,1,0:T(8,128)}), f32[1,128,3200]{2,1,0:T(8,128)}) %reduce-scatter.23.cloned.1.call-update) | async-done | bytes 1638416
  597.4 70.9 %reduce-scatter.25.cloned.1.call-done = f32[1,128,3200]{2,1,0:T(8,128)} async-done(((f32[1,1024,3200]{2,1,0:T(8,128)}), f32[1,128,3200]{2,1,0:T(8,128)}) %reduce-scatter.25.cloned.1.call-update) | async-done | bytes 1638416
  669.8 6.0 fusion.122
  675.8 60.0 %all-gather.14.cloned.1.call-done = bf16[1,2,3200,1024]{3,2,1,0:T(8,128)(2,1)} async-done(((bf16[1,2,400,1024]{3,2,1,0:T(8,128)(2,1)}), bf16[1,2,3200,1024]{3,2,1,0:T(8,128)(2,1)}) %all-gather.14.cloned.1.call-update) | async-done | bytes 13107216 | tf_op jit(solution)/reshape | solution.py:52
  735.9 68.1 %all-gather.10.cloned.1.call-done = bf16[1,2,1024,3200]{3,2,1,0:T(8,128)(2,1)} async-done(((bf16[1,2,128,3200]{3,2,1,0:T(8,128)(2,1)}), bf16[1,2,1024,3200]{3,2,1,0:T(8,128)(2,1)}) %all-gather.10.cloned.1.call-update) | async-done | bytes 13107216 | tf_op jit(solution)/reshape | solution.py:52
  803.9 68.1 %all-gather.12.cloned.1.call-done = bf16[1,2,1024,3200]{3,2,1,0:T(8,128)(2,1)} async-done(((bf16[1,2,128,3200]{3,2,1,0:T(8,128)(2,1)}), bf16[1,2,1024,3200]{3,2,1,0:T(8,128)(2,1)}) %all-gather.12.cloned.1.call-update) | async-done | bytes 13107216 | tf_op jit(solution)/reshape | solution.py:52
  872.0 12.7 %copy.5 = bf16[2,1024,3200]{2,1,0:T(8,128)(2,1)} copy(bf16[2,1024,3200]{2,1,0:T(8,128)(2,1)} %bitcast.332) | data formatting | bytes 26214400
  884.7 6.6 copy.6
  (83 shorter events, 27.2 us)
Async XLA Ops:
  7.2 424.9 %reduce-scatter.27.cloned.1.call-start = ((), (), s32[]{:S(2)}) async-start(), calls=%async_computation.13 | async-start | bytes 14745600
  10.3 28.6 %slice-start.4 = ((s8[13107200]{0:T(1024)(128)(4,1)}), s8[524288]{0:T(1024)(128)(4,1)S(1)}, s32[]{:S(2)}) async-start(s8[13107200]{0:T(1024)(128)(4,1)} %bitcast.334), calls=%async_computation.19 | async-start | bytes 1048576
  16.9 22.1 %copy-start.13 = (f32[2048]{0:T(1024)}, f32[2048]{0:T(1024)S(1)}, u32[]{:S(2)}) copy-start(f32[2048]{0:T(1024)S(1)} %add_rsqrt_fusion) | copy-start | bytes 24580
  16.9 22.1 %copy-start.1 = (bf16[1,2048,1024]{2,1,0:T(8,128)(2,1)S(1)}, bf16[1,2048,1024]{2,1,0:T(8,128)(2,1)}, u32[]{:S(2)}) copy-start(bf16[1,2048,1024]{2,1,0:T(8,128)(2,1)} %param.2) | copy-start | bytes 12582916
  16.9 22.1 %slice-start.5 = ((s8[13107200]{0:T(1024)(128)(4,1)}), s8[4194304]{0:T(1024)(128)(4,1)S(1)}, s32[]{:S(2)}) async-start(s8[13107200]{0:T(1024)(128)(4,1)} %bitcast.334), calls=%async_computation.20 | async-start | bytes 8388608
  17.0 22.0 %slice-start.6 = ((s8[13107200]{0:T(1024)(128)(4,1)}), s8[4194304]{0:T(1024)(128)(4,1)S(1)}, s32[]{:S(2)}) async-start(s8[13107200]{0:T(1024)(128)(4,1)} %bitcast.334), calls=%async_computation.21 | async-start | bytes 8388608
  17.0 22.0 %slice-start.7 = ((s8[13107200]{0:T(1024)(128)(4,1)}), s8[4194304]{0:T(1024)(128)(4,1)S(1)}, s32[]{:S(2)}) async-start(s8[13107200]{0:T(1024)(128)(4,1)} %bitcast.334), calls=%async_computation.22 | async-start | bytes 8388608
  102.2 23.9 %copy-start.11 = (f32[1,1,2048]{2,1,0:T(1,128)}, f32[1,1,2048]{2,1,0:T(1,128)S(1)}, u32[]{:S(2)}) copy-start(f32[1,1,2048]{2,1,0:T(1,128)S(1)} %rsqrt.31) | copy-start | bytes 24580
  102.7 23.4 %copy-start.3 = (bf16[1,1,2048,1024]{2,3,1,0:T(8,128)(2,1)S(1)}, bf16[1,1,2048,1024]{2,3,1,0:T(8,128)(2,1)}, u32[]{:S(2)}) copy-start(bf16[1,1,2048,1024]{2,3,1,0:T(8,128)(2,1)} %get-tuple-element.10) | copy-start | bytes 12582916
  175.4 259.1 %reduce-scatter.29.cloned.1.call-start = ((), (), s32[]{:S(2)}) async-start(), calls=%async_computation.14 | async-start | bytes 14745600
  252.2 23.3 %copy-start.10 = (f32[2048]{0:T(1024)S(1)}, f32[2048]{0:T(1024)}, u32[]{:S(2)}) copy-start(f32[2048]{0:T(1024)} %copy-done.9) | copy-start | bytes 24580
  252.2 23.4 %copy-start = (bf16[1,2048,1024]{1,2,0:T(8,128)(2,1)S(1)}, bf16[1,2048,1024]{1,2,0:T(8,128)(2,1)}, u32[]{:S(2)}) copy-start(bf16[1,2048,1024]{1,2,0:T(8,128)(2,1)} %copy.1) | copy-start | bytes 12582916
  252.2 23.4 %copy-start.12 = (f32[1,1,2048]{2,1,0:T(1,128)S(1)}, f32[1,1,2048]{2,1,0:T(1,128)}, u32[]{:S(2)}) copy-start(f32[1,1,2048]{2,1,0:T(1,128)} %copy-done.11) | copy-start | bytes 24580
  280.9 2.0 copy-start.4
  302.6 146.3 %reduce-scatter.19.cloned.1.call-start = ((), (), s32[]{:S(2)}) async-start(), calls=%async_computation.9 | async-start | bytes 14745600
  324.8 21.3 %copy-start.14 = (f32[2048]{0:T(1024)S(1)}, f32[2048]{0:T(1024)}, u32[]{:S(2)}) copy-start(f32[2048]{0:T(1024)} %copy-done.13) | copy-start | bytes 24580
  324.8 197.4 %reduce-scatter.21.cloned.1.call-start = ((), (), s32[]{:S(2)}) async-start(), calls=%async_computation.10 | async-start | bytes 14745600
  324.9 21.2 %copy-start.5 = (bf16[1,2048,1024]{1,2,0:T(8,128)(2,1)S(1)}, bf16[1,2048,1024]{1,2,0:T(8,128)(2,1)}, u32[]{:S(2)}) copy-start(bf16[1,2048,1024]{1,2,0:T(8,128)(2,1)} %copy) | copy-start | bytes 12582916
  378.1 216.9 %reduce-scatter.23.cloned.1.call-start = ((), (), s32[]{:S(2)}) async-start(), calls=%async_computation.11 | async-start | bytes 14745600
  404.3 264.0 %reduce-scatter.25.cloned.1.call-start = ((), (), s32[]{:S(2)}) async-start(), calls=%async_computation.12 | async-start | bytes 14745600
  430.1 0.7 copy-start.15
  430.2 5.9 copy-start.6
  430.2 305.6 %all-gather.14.cloned.1.call-start = ((), (), s32[]{:S(2)}) async-start(), calls=%async_computation.8 | async-start | bytes 14745600 | tf_op jit(solution)/reshape | solution.py:52
  442.3 81.5 %copy-start.7 = (f32[2,128,3200]{2,1,0:T(8,128)S(1)}, f32[2,128,3200]{2,1,0:T(8,128)}, u32[]{:S(2)}) copy-start(f32[2,128,3200]{2,1,0:T(8,128)} %param.6) | copy-start | bytes 9830404
  442.4 361.5 %all-gather.10.cloned.1.call-start = ((), (), s32[]{:S(2)}) async-start(), calls=%async_computation.6 | async-start | bytes 14745600 | tf_op jit(solution)/reshape | solution.py:52
  529.8 140.0 %copy-start.8 = (f32[2,128,3200]{2,1,0:T(8,128)S(1)}, f32[2,128,3200]{2,1,0:T(8,128)}, u32[]{:S(2)}) copy-start(f32[2,128,3200]{2,1,0:T(8,128)} %param.8) | copy-start | bytes 9830404
  529.8 342.2 %all-gather.12.cloned.1.call-start = ((), (), s32[]{:S(2)}) async-start(), calls=%async_computation.7 | async-start | bytes 14745600 | tf_op jit(solution)/reshape | solution.py:52
  872.0 12.7 %copy-start.2 = (bf16[1,2,1024,3200]{3,2,1,0:T(8,128)(2,1)S(1)}, bf16[1,2,1024,3200]{3,2,1,0:T(8,128)(2,1)}, u32[]{:S(2)}) copy-start(bf16[1,2,1024,3200]{3,2,1,0:T(8,128)(2,1)} %all-gather.12.cloned.1.call-done) | copy-start | bytes 39321604
  872.0 19.4 %slice-start = ((s8[13107200]{0:T(1024)(128)(4,1)}), s8[4194304]{0:T(1024)(128)(4,1)S(1)}, s32[]{:S(2)}) async-start(s8[13107200]{0:T(1024)(128)(4,1)} %bitcast.329), calls=%async_computation.15 | async-start | bytes 8388608
  872.0 20.5 %slice-start.1 = ((s8[13107200]{0:T(1024)(128)(4,1)}), s8[4194304]{0:T(1024)(128)(4,1)S(1)}, s32[]{:S(2)}) async-start(s8[13107200]{0:T(1024)(128)(4,1)} %bitcast.329), calls=%async_computation.16 | async-start | bytes 8388608
  884.7 9.1 %slice-start.2 = ((s8[13107200]{0:T(1024)(128)(4,1)}), s8[4194304]{0:T(1024)(128)(4,1)S(1)}, s32[]{:S(2)}) async-start(s8[13107200]{0:T(1024)(128)(4,1)} %bitcast.329), calls=%async_computation.17 | async-start | bytes 8388608
  884.7 9.1 %slice-start.3 = ((s8[13107200]{0:T(1024)(128)(4,1)}), s8[524288]{0:T(1024)(128)(4,1)S(1)}, s32[]{:S(2)}) async-start(s8[13107200]{0:T(1024)(128)(4,1)} %bitcast.329), calls=%async_computation.18 | async-start | bytes 1048576
  (1 other events, 0.6 us)
Sparse Core Ops, SparseCore 0:
  175.6 73.3 reduce-scatter.26
  302.8 73.3 reduce-scatter.28
  378.4 70.5 reduce-scatter.18
  451.7 70.5 reduce-scatter.20
  524.4 70.5 reduce-scatter.22
  597.7 70.5 reduce-scatter.24
  669.8 65.9 all-gather.13
  738.0 65.8 all-gather.9
  806.1 65.8 all-gather.11
where the time goes:
time: 913 us; the launch traced here: 906 us
  waiting for transfers between devices  410 us (45%)
  matrix products  348 us (38%)
  other arithmetic  88.2 us (10%)
  local copies, waits for them, and re-layouts  43.6 us (5%)
  between operations  15.2 us (2%)
    unnamed x15, waiting for transfers between devices  214 us
    reshape x3, waiting for transfers between devices, step(): t.reshape(-1, *t.shape[2:])  196 us
    dot_general x5, matrix products, layer(): gate = jnp.dot(a, w['w_gate'], preferred_element_type=jnp.float32)  123 us
    dot_general x5, matrix products, layer(): up = jnp.dot(a, w['w_up'], preferred_element_type=jnp.float32)  113 us
    dot_general x5, matrix products, matmul(): jnp.dot(a, w, preferred_element_type=jnp.float32).astype(jnp.bfloat16)  112 us
    unnamed x5, other arithmetic  55.1 us
    unnamed x53, local copies, waits for them, and re-layouts  43 us
  transfers between devices with their start and end apart: 9, of which 7 were waited for; matrix products, arithmetic and copies ran while one was open for 31% of the time, Pallas kernels for 0%

commit v1 on v0

v1 whole, which is shorter than its diff:
```python
import functools

import jax
import jax.numpy as jnp
from jax import lax
from jax.experimental import pallas as pl
from jax.experimental.pallas import tpu as pltpu
from jax.sharding import PartitionSpec as P

F32, BF16 = jnp.float32, jnp.bfloat16
PIECES = 5
TILE = 512
MESH = pl.DeviceIdType.MESH


def dot(a, b, ca=1, cb=0):
    return lax.dot_general(a, b, (((ca,), (cb,)), ((), ())), preferred_element_type=F32)


def norm(h):
    wide = h.astype(F32)
    scale = lax.rsqrt(jnp.mean(wide * wide, -1, keepdims=True) + 1e-6)
    return (wide * scale).astype(BF16)


def new_moments(m, v, g):
    return 0.9 * m + 0.1 * g, 0.95 * v + 0.05 * g * g


class Kind:
    pass


def wide_sum(*parts):
    total = parts[0].astype(F32)
    for part in parts[1:]:
        total = total + part.astype(F32)
    return total


def kernel(dims, *refs):
    T, D, FF, C, R, RB, PB = dims
    it = iter(refs)
    take = lambda n: [next(it) for _ in range(n)]
    a1, a1t, dy, dyt, h1, a0, a0t = take(7)
    wg, wu, wd, mg, mu, md, vg, vu, vd = take(9)
    nw_a, nw_b, g_a, g_b, dwd = take(5)
    a, at, d, dt, da, wgc, wuc, wdc, act, dgate, dup, dwdc, grad = take(13)
    load_sem, w_sem, dwd_sem = take(3)
    kinds = []
    for name in "ab":
        k = Kind()
        k.name = name
        k.dd, k.s1, k.r1, k.s2, k.r2, k.m, k.v, k.w, k.nw, k.g = take(10)
        k.dd_s, k.dd_r, k.s1_s, k.s1_r, k.s2_s, k.s2_r = take(6)
        k.ax_s, k.ax_r, k.ah_s, k.ah_r, k.ad_s, k.ad_r, k.st_sem, k.out_sem = take(8)
        kinds.append(k)
    ka, kb = kinds
    kb.own, kb.own_sem = take(2)
    assert next(it, None) is None

    me = lax.axis_index("dp")
    chip, core = me // 2, me % 2
    other = 1 - core
    right, left, across = (chip + 1) % 4, (chip + 3) % 4, (chip + 2) % 4
    partner = chip * 2 + other
    to = (right * 2 + core, left * 2 + core)
    frm = (left, right)

    barrier = pltpu.get_barrier_semaphore()
    for peer in (partner, *to):
        pl.semaphore_signal(barrier, inc=1, device_id={"dp": peer}, device_id_type=MESH)
    pl.semaphore_wait(barrier, 3)

    def remote(src, dst, send, recv, peer):
        return pltpu.make_async_remote_copy(src_ref=src, dst_ref=dst, send_sem=send, recv_sem=recv,
                                            device_id={"dp": peer}, device_id_type=MESH)

    local = pltpu.make_async_copy
    aligned = lambda i, n: pl.ds(pl.multiple_of(i * n, n), n)

    ka.na, ka.r, ka.n, ka.half = 2, R, C, (2, R // 2, C)
    kb.na, kb.r, kb.n, kb.half = 1, PB, D, (1, PB, D // 2)
    ka.first, kb.first = 0, PIECES
    for k in kinds:
        k.where = lambda s, k=k: (1 - (s - k.first) // PIECES, (s - k.first) % PIECES)

    def own_a(s, y):
        return grad.at[s % 2, :, y, core]

    ka.tile = own_a
    kb.tile = lambda s, y: kb.own.at[s % 2, :, y]

    def out_a(s, j):
        layer, c = ka.where(s)
        return nw_a.at[layer, :, aligned(j, R), aligned(c, C)]

    def out_half_a(s, j, h):
        layer, c = ka.where(s)
        return nw_a.at[layer, :, pl.ds(pl.multiple_of(j * R + h * (R // 2), R // 2), R // 2), aligned(c, C)]

    def rows_b(j, p):
        return pl.ds(pl.multiple_of(j * RB + p * PB, PB), PB)

    def out_b(s, j):
        layer, p = kb.where(s)
        return nw_b.at[pl.ds(layer, 1), rows_b(j, p)]

    def out_half_b(s, j, h):
        layer, p = kb.where(s)
        return nw_b.at[pl.ds(layer, 1), rows_b(j, p), pl.ds(h * (D // 2), D // 2)]

    ka.out, ka.out_half, kb.out, kb.out_half = out_a, out_half_a, out_b, out_half_b
    ka.half_of = lambda ref, h: ref.at[:, pl.ds(h * (R // 2), R // 2), :]
    kb.half_of = lambda ref, h: ref.at[:, :, pl.ds(h * (D // 2), D // 2)]

    def state_copies(k, s):
        layer, c = k.where(s)
        if k is ka:
            cols = aligned(c, C)
            out = []
            for i, (w, m, v) in enumerate(((wg, mg, vg), (wu, mu, vu))):
                out += [local(w.at[layer, aligned(me, R), cols], k.w.at[i], k.st_sem.at[3 * i]),
                        local(m.at[layer, :, cols], k.m.at[i], k.st_sem.at[3 * i + 1]),
                        local(v.at[layer, :, cols], k.v.at[i], k.st_sem.at[3 * i + 2])]
            return out
        rows = aligned(c, PB)
        one = pl.ds(layer, 1)
        return [local(wd.at[one, rows_b(me, c)], k.w, k.st_sem.at[0]),
                local(md.at[one, rows], k.m, k.st_sem.at[1]), local(vd.at[one, rows], k.v, k.st_sem.at[2])]

    def g_out(k, s):
        layer, c = k.where(s)
        return g_a.at[layer, :, :, aligned(c, C)] if k is ka else g_b.at[pl.ds(layer, 1), aligned(c, PB)]

    def own_copy(k, s):
        return (local(k.nw.at[s % 2], k.out(s, me), k.out_sem.at[s % 2, 0]),
                local(k.g.at[s % 2], g_out(k, s), k.out_sem.at[s % 2, 1]))

    def dd_copy(k, s):
        return remote(grad.at[s % 2, :, :, other], k.dd.at[s % 2], k.dd_s.at[s % 2], k.dd_r.at[s % 2], partner)

    def s1_copy(k, s, h):
        return remote(k.half_of(k.s1.at[s % 2], h), k.r1.at[s % 2, h], k.s1_s.at[s % 2, h], k.s1_r.at[s % 2, h], to[h])

    def s2_copy(k, s, h):
        return remote(k.s2.at[s % 2, h], k.r2.at[s % 2, h], k.s2_s.at[s % 2, h], k.s2_r.at[s % 2, h], to[h])

    def ax_copy(k, s, h):
        return remote(k.nw.at[s % 2], k.out(s, me), k.ax_s.at[s % 4, h], k.ax_r.at[s % 4, h], to[h])

    def ax_wait(k, s, h):
        j = frm[h] * 2 + core
        return remote(k.out(s, j), k.out(s, j), k.ax_s.at[s % 4, h], k.ax_r.at[s % 4, h], to[h])

    def ah_copy(k, s, h):
        src = k.out_half(s, frm[h] * 2 + core, h)
        return remote(src, src, k.ah_s.at[s % 4, h], k.ah_r.at[s % 4, h], to[h])

    def ah_wait(k, s, h):
        src = k.out_half(s, across * 2 + core, h)
        return remote(src, src, k.ah_s.at[s % 4, h], k.ah_r.at[s % 4, h], to[h])

    def ad_copy(k, s, i):
        if i == 0:
            return remote(k.nw.at[s % 2], k.out(s, me), k.ad_s.at[s % 4, 0], k.ad_r.at[s % 4, 0], partner)
        y = (chip, left, right, across)[i]
        src = k.out(s, y * 2 + core)
        return remote(src, src, k.ad_s.at[s % 4, i], k.ad_r.at[s % 4, i], partner)

    def ad_wait(k, s, i):
        y = (chip, left, right, across)[i]
        src = k.out(s, y * 2 + other)
        return remote(src, src, k.ad_s.at[s % 4, i], k.ad_r.at[s % 4, i], partner)

    def blocks(k, body):
        rows, cols = k.half[1], k.half[2]
        for h in range(2):
            @pl.loop(0, rows // 16)
            def _(i):
                if k is ka:
                    cut = lambda ref: ref.at[:, pl.ds(pl.multiple_of(h * rows + i * 16, 16), 16), :]
                else:
                    cut = lambda ref: ref.at[:, pl.ds(pl.multiple_of(i * 16, 16), 16), pl.ds(h * cols, cols)]
                cut_half = lambda ref: ref.at[:, pl.ds(pl.multiple_of(i * 16, 16), 16), :]
                body(cut, cut_half, h)

    def stage_a(k, s):
        if k is ka:
            dd_copy(k, s).start()
            return
        layer, p = k.where(s)
        for y in range(4):
            local(dwd.at[layer, pl.ds((y * 2 + core) * PIECES + p, 1)], k.own.at[s % 2, :, y], k.own_sem.at[s % 2]).start()
            remote(dwd.at[layer, pl.ds((y * 2 + other) * PIECES + p, 1)], k.dd.at[s % 2, :, y],
                   k.dd_s.at[s % 2], k.dd_r.at[s % 2], partner).start()

    def dd_wait(k, s):
        return remote(k.dd.at[s % 2], k.dd.at[s % 2], k.dd_s.at[s % 2], k.dd_r.at[s % 2], partner)

    def stage_b(k, s):
        slot = s % 2
        dd_wait(k, s).wait_recv()
        if k is kb:
            local(k.own.at[slot], k.own.at[slot], k.own_sem.at[slot]).wait()
        mine, theirs = k.tile(s, across), k.dd.at[slot, :, across]

        def body(cut, cut_half, h):
            cut(k.s1.at[slot])[...] = wide_sum(cut(mine)[...], cut(theirs)[...]).astype(BF16)

        blocks(k, body)
        for h in range(2):
            s1_copy(k, s, h).start()
        for c in state_copies(k, s):
            c.start()

    def stage_c(k, s):
        slot = s % 2
        for h in range(2):
            s1_copy(k, s, h).wait_recv()
        for way in range(2):
            y = (right, left)[way]
            mine, theirs = k.tile(s, y), k.dd.at[slot, :, y]

            def body(cut, cut_half, h):
                parts = [cut(mine)[...], cut(theirs)[...]]
                if h == way:
                    parts.append(cut_half(k.r1.at[slot, way])[...])
                cut(k.s2.at[slot, way])[...] = wide_sum(*parts).astype(BF16)

            blocks(k, body)
            s2_copy(k, s, way).start()
        for h in range(2):
            s1_copy(k, s, h).wait_send()
        dd_wait(k, s).wait_send()

    def stage_d(k, s):
        slot = s % 2
        for c in state_copies(k, s):
            c.wait()
        for h in range(2):
            s2_copy(k, s, h).wait_recv()
        mine, theirs = k.tile(s, chip), k.dd.at[slot, :, chip]

        def body(cut, cut_half, h):
            g = wide_sum(cut(mine)[...], cut(theirs)[...], cut(k.r2.at[slot, 0])[...], cut(k.r2.at[slot, 1])[...]).astype(BF16)
            cut(k.g.at[slot])[...] = g
            m, v = new_moments(cut(k.m)[...], cut(k.v)[...], g.astype(F32))
            w = cut(k.w)[...].astype(F32)
            cut(k.nw.at[slot])[...] = (w - 0.02 * (m * lax.rsqrt(v + 1e-8) + 0.1 * w)).astype(BF16)

        blocks(k, body)
        for h in range(2):
            ax_copy(k, s, h).start()
        ad_copy(k, s, 0).start()
        for c in own_copy(k, s):
            c.start()
        for h in range(2):
            s2_copy(k, s, h).wait_send()

    def stage_e(k, s):
        for h in range(2):
            ax_wait(k, s, h).wait_recv()
            ah_copy(k, s, h).start()
            ad_copy(k, s, 1 + h).start()
        ad_wait(k, s, 0).wait_recv()
        for c in own_copy(k, s):
            c.wait()
        for h in range(2):
            ax_copy(k, s, h).wait_send()
        ad_copy(k, s, 0).wait_send()

    def stage_f(k, s):
        for h in range(2):
            ah_wait(k, s, h).wait_recv()
        ad_copy(k, s, 3).start()

    def stage_g(k, s):
        for i in range(1, 4):
            ad_wait(k, s, i).wait_recv()
        for h in range(2):
            ah_copy(k, s, h).wait_send()
        for i in range(1, 4):
            ad_copy(k, s, i).wait_send()

    def run(stage, k, s, base):
        @pl.when((s >= k.first) & (s < k.first + 2 * PIECES))
        def _():
            stage(k, s)

    def early(s, here):
        for k in here:
            run(stage_f, k, s - 2, 0)
        for k in here:
            run(stage_d, k, s - 1, 0)
        for k in here:
            run(stage_a, k, s, 0)

    def late(s, here):
        for k in here:
            run(stage_b, k, s, 0)

    def even(s, here):
        for k in here:
            run(stage_e, k, s - 1, 0)
        for k in here:
            run(stage_c, k, s, 0)
        for k in here:
            run(stage_g, k, s - 2, 0)

    def weight_copies(layer, c):
        return (local(wg.at[layer, :, aligned(c, C)], wgc, w_sem.at[0]), local(wu.at[layer, :, aligned(c, C)], wuc, w_sem.at[1]),
                local(wd.at[layer, aligned(c, C)], wdc, w_sem.at[2]))

    def dwd_copy(layer, c):
        return local(dwdc, dwd.at[layer, pl.ds(c * 8, 8)], dwd_sem)

    def chunks(layer, here):
        first = (1 - layer) * PIECES

        @pl.loop(0, PIECES)
        def _(c):
            s = c + first
            for copy in weight_copies(layer, c):
                copy.wait()

            def tokens(i):
                rows = aligned(i, TILE)
                gate = dot(a[rows, :], wgc[...])
                up = dot(a[rows, :], wuc[...])
                dact = dot(d[rows, :], wdc[...], 1, 1).astype(BF16).astype(F32)
                sig = jax.nn.sigmoid(gate)
                silu = gate * sig
                act[rows, :] = (silu * up).astype(BF16)
                dup[rows, :] = (dact * silu).astype(BF16)
                dgate[rows, :] = (dact * up * (sig * (1 + gate * (1 - sig)))).astype(BF16)
                if layer:
                    more = dot(dgate[rows, :], wgc[...], 1, 1) + dot(dup[rows, :], wuc[...], 1, 1)

                    @pl.when(c == 0)
                    def _():
                        da[rows, :] = more

                    @pl.when(c > 0)
                    def _():
                        da[rows, :] += more

            half = T // TILE // 2
            pl.loop(0, half)(tokens)
            even(s - 1, here)
            pl.loop(half, 2 * half)(tokens)

            @pl.when(c < PIECES - 1)
            def _():
                for copy in weight_copies(layer, c + 1):
                    copy.start()

            for i, by in enumerate((dgate, dup)):
                @pl.loop(0, 2)
                def _(j):
                    block = dot(at[aligned(j, D // 2), :], by[...]).astype(BF16)
                    grad[s % 2, i, pl.ds(j * 2, 2)] = block.reshape(2, 2, R, C)

            early(s, here)

            @pl.when(c > 0)
            def _():
                dwd_copy(layer, c - 1).wait()

            for j in range(4):
                block = dot(dt[j * (D // 4) : (j + 1) * (D // 4), :], act[...]).astype(BF16)
                dwdc[:, :, j * (D // 4) : (j + 1) * (D // 4)] = block.T.reshape(8, PB, D // 4)
            dwd_copy(layer, c).start()
            late(s, here)

        dwd_copy(layer, PIECES - 1).wait()

    top = [local(src, dst, load_sem.at[i]) for i, (src, dst) in enumerate(((a1, a), (a1t, at), (dy, d), (dyt, dt)))]
    for copy in (*top, *weight_copies(1, 0)):
        copy.start()
    for copy in top:
        copy.wait()
    chunks(1, (ka,))

    bring = local(h1, a, load_sem.at[0])
    bring.start()
    low_t = local(a0t, at, load_sem.at[1])
    low_t.start()
    for copy in weight_copies(0, 0):
        copy.start()
    bring.wait()

    @pl.loop(0, T // 256)
    def _(i):
        rows = aligned(i, 256)
        wide = a[rows, :].astype(F32)
        scale = lax.rsqrt(jnp.mean(wide * wide, -1, keepdims=True) + 1e-6)
        by = da[rows, :].astype(BF16).astype(F32)
        inner = jnp.mean(wide * by, -1, keepdims=True)
        through = (by * scale - wide * (inner * scale * scale * scale)).astype(BF16)
        total = d[rows, :] + through
        d[rows, :] = total
        dt[:, rows] = total.T

    low = local(a0, a, load_sem.at[0])
    low.start()
    low.wait()
    low_t.wait()
    chunks(0, (ka, kb))

    @pl.loop(2 * PIECES, 3 * PIECES + 3)
    def _(s):
        even(s - 1, (ka, kb))
        early(s, (ka, kb))
        late(s, (ka, kb))


def gathered_step(mesh, dims, operands):
    T, D, FF, C, R, RB, PB = dims
    hbm = pl.BlockSpec(memory_space=pl.ANY)
    vmem, dma = pltpu.VMEM, pltpu.SemaphoreType.DMA
    shapes = [vmem((T, D), BF16), vmem((D, T), BF16), vmem((T, D), BF16), vmem((D, T), BF16), vmem((T, D), F32)]
    shapes += [vmem((D, C), BF16), vmem((D, C), BF16), vmem((C, D), BF16)]
    shapes += [vmem((T, C), BF16)] * 3 + [vmem((8, PB, D), BF16), vmem((2, 2, 4, 2, R, C), BF16)]
    shapes += [dma((4,)), dma((3,)), dma]
    for na, r, n, half in ((2, R, C, (2, R // 2, C)), (1, PB, D, (1, PB, D // 2))):
        tile = (na, r, n)
        shapes += [vmem((2, na, 4, r, n), BF16), vmem((2, *tile), BF16), vmem((2, 2, *half), BF16), vmem((2, 2, *tile), BF16),
                   vmem((2, 2, *tile), BF16), vmem(tile, F32), vmem(tile, F32), vmem(tile, BF16), vmem((2, *tile), BF16),
                   vmem((2, *tile), BF16)]
        shapes += [dma((2,)), dma((2,)), dma((2, 2)), dma((2, 2)), dma((2, 2)), dma((2, 2))]
        shapes += [dma((4, 2)), dma((4, 2)), dma((4, 2)), dma((4, 2)), dma((4, 4)), dma((4, 4)), dma((6,)), dma((2, 2))]
    shapes += [vmem((2, 1, 4, PB, D), BF16), dma((2,))]
    out = lambda *s: jax.ShapeDtypeStruct(s, BF16)
    L = 2
    return pl.pallas_call(
        functools.partial(kernel, dims),
        out_shape=(out(L, 2, D, FF), out(L, FF, D), out(L, 2, R, FF), out(L, RB, D), out(L, 8 * PIECES, PB, D)),
        in_specs=[hbm] * len(operands),
        out_specs=(hbm,) * 5,
        scratch_shapes=shapes,
        compiler_params=pltpu.CompilerParams(collective_id=0, has_side_effects=True, vmem_limit_bytes=67_000_000),
        name="backward_and_update",
    )(*operands)


def solution(mesh):
    assert mesh.shape["dp"] == 8

    def body(x, dy, wg, wu, wd, mg, mu, md, vg, vu, vd):
        T, D = x.shape[1:]
        FF = wg.shape[2]
        dims = (T, D, FF, FF // PIECES, D // 8, FF // 8, FF // 8 // PIECES)
        x, dy = x[0], dy[0]
        a0 = norm(x)
        gate = dot(a0, wg[0])
        up = dot(a0, wu[0])
        h1 = x + dot((jax.nn.silu(gate) * up).astype(BF16), wd[0]).astype(BF16)
        a1 = norm(h1)
        operands = (a1, a1.T, dy, dy.T, h1, a0, a0.T, wg, wu, wd, mg, mu, md, vg, vu, vd)
        nw_a, nw_b, g_a, g_b, _ = gathered_step(mesh, dims, operands)
        g = [g_a[:, 0], g_a[:, 1], g_b]
        new = [new_moments(m, v, t.astype(F32)) for m, v, t in zip((mg, mu, md), (vg, vu, vd), g, strict=True)]
        return (nw_a[:, 0], nw_a[:, 1], nw_b, *(t[0] for t in new), *(t[1] for t in new))

    seq, rep, rows = P(("rep", "dp")), P(), P(None, "dp")
    return jax.shard_map(
        body, mesh=mesh, in_specs=(seq, seq, rep, rep, rep) + (rows,) * 6,
        out_specs=(P("rep"),) * 3 + (P("rep", "dp"),) * 6, check_vma=False)
```

time: 913 us -> 630 us (0.69)
  Pallas kernels: 0 us -> 460 us
  waiting for transfers between devices: 410 us -> 0 us
  matrix products: 348 us -> 67.9 us
  other arithmetic: 88.2 us -> 31.8 us
  local copies, waits for them, and re-layouts: 43.6 us -> 60.1 us
  between operations: 15.2 us -> 1.19 us
    pallas_call x0 -> x1, Pallas kernels: none -> 460 us  [gathered_step(): pl.pallas_call(functools.partial(kernel, dims), out_shape=(out(L, 2, D, F...]
    dot_general x15 -> x3, matrix products: 348 us -> 67.9 us  [dot(): lax.dot_general(a, b, (((ca,), (cb,)), ((), ())), preferred_element_type=...]
    unnamed x15 -> x0, waiting for transfers between devices: 214 us -> none
    reshape x3 -> x0, waiting for transfers between devices: 196 us -> none  [step(): t.reshape(-1, *t.shape[2:])]
    unnamed x5 -> x1, other arithmetic: 55.1 us -> 0.01 us
    unnamed x53 -> x29, local copies, waits for them, and re-layouts: 43 us -> 21.2 us
    squeeze x0 -> x1, local copies, waits for them, and re-layouts: none -> 19.7 us  [body(): nw_a[:, 1]]
    reshape x3 -> x0, other arithmetic: 18.2 us -> none  [step(): t.reshape(-1, *t.shape[2:])]
  transfers between devices with their start and end apart: 9 -> 0, of which waited for: 7 -> 0; matrix products, arithmetic and copies ran while one was open for 31% -> 0% of each run, Pallas kernels for 0% -> 0%
where the time goes in v1:
time: 630 us; the launch traced here: 621 us
  Pallas kernels  460 us (73%)
  matrix products  67.9 us (11%)
  local copies, waits for them, and re-layouts  60.1 us (10%)
  other arithmetic  31.8 us (5%)
    pallas_call x1, Pallas kernels, gathered_step(): pl.pallas_call(functools.partial(kernel, dims), out_shape=(out(L, 2, D, F...  460 us
    dot_general x3, matrix products, dot(): lax.dot_general(a, b, (((ca,), (cb,)), ((), ())), preferred_element_type=...  67.9 us
    unnamed x29, local copies, waits for them, and re-layouts  21.2 us
    squeeze x1, local copies, waits for them, and re-layouts, body(): nw_a[:, 1]  19.7 us
    add x2, other arithmetic, new_moments(): return (0.9 * m + 0.1 * g, 0.95 * v + 0.05 * g * g)  13.2 us
    convert_element_type x2, local copies, waits for them, and re-layouts, norm(): return (wide * scale).astype(BF16)  12.8 us

profile of v1, /device:TPU:113, one launch (start us, length us, event | category | flops | bytes accessed | tf_op | source)
XLA Modules:
  0.0 620.8 jit_solution(11088528866847728663)
XLA Ops:
  0.6 6.4 %copy.20 = bf16[1,2048,1024]{1,2,0:T(8,128)(2,1)} copy(bf16[1,2048,1024]{2,1,0:T(8,128)(2,1)} %param.11) | data formatting | bytes 8388608 | tf_op args[0]
  7.1 3.2 fusion
  10.3 0.2 copy-done
  10.5 3.3 fusion.33.refs_6_
  13.8 3.2 fusion.1
  17.0 6.5 %copy.25.refs_5_ = bf16[2048,1024]{1,0:T(8,128)(2,1)} copy(bf16[2048,1024]{0,1:T(8,128)(2,1)} %fusion.1) | data formatting | bytes 8388608 | tf_op jit(solution)/shard_map/convert_element_type | solution.py:23
  23.5 6.5 %copy.21 = bf16[1,2048,1024]{1,2,0:T(8,128)(2,1)} copy(bf16[1,2048,1024]{2,1,0:T(8,128)(2,1)} %param.12) | data formatting | bytes 8388608 | tf_op args[1]
  30.0 21.8 %fusion.8 = f32[2048,3200]{1,0:T(8,128)} fusion(bf16[2,1024,3200]{2,1,0:T(8,128)(2,1)} %refs_7_.1, bf16[1,2048,1024]{2,1,0:T(8,128)(2,1)} %param.11, f32[2048]{0:T(1024)S(1)} %add_rsqrt_fusion.1), kind=kOutput, calls=%fused_computation.15 | convolution fusion | flops 13428064256 | bytes 36970496 | tf_op jit(solution)/shard_map/dot_general | solution.py:17
  51.8 23.7 %multiply_convert_fusion.clone.3.clone.5 = bf16[2048,3200]{1,0:T(8,128)(2,1)} fusion(f32[2048,3200]{1,0:T(8,128)} %fusion.8, bf16[2,1024,3200]{2,1,0:T(8,128)(2,1)} %refs_8_.1, bf16[1,2048,1024]{2,1,0:T(8,128)(2,1)} %param.11, f32[2048]{0:T(1024)S(1)} %add_rsqrt_fusion.1), kind=kOutput, calls=%fused_computation.clone.clone.clone.clone.clone.clone.clone.2 | convolution fusion | flops 13467385856 | bytes 50077696 | tf_op jit(solution)/shard_map/dot_general | solution.py:17
  75.5 22.3 %fusion.2 = (f32[2048]{0:T(1024)S(1)}, bf16[2048,1024]{0,1:T(8,128)(2,1)}) fusion(bf16[2,3200,1024]{2,1,0:T(8,128)(2,1)} %refs_9_.1, bf16[1,2048,1024]{1,2,0:T(8,128)(2,1)} %copy.20, bf16[2048,3200]{1,0:T(8,128)(2,1)} %multiply_convert_fusion.clone.3.clone.5), kind=kOutput, calls=%fused_computation.9 | convolution fusion | flops 13432256512 | bytes 28057600 | tf_op jit(solution)/shard_map/dot_general | solution.py:17
  97.8 0.0 copy-start.1
  97.8 5.7 fusion.34.refs_1_
  103.5 3.2 fusion.3
  106.7 6.4 %copy.24.refs_4_ = bf16[2048,1024]{1,0:T(8,128)(2,1)} copy(bf16[2048,1024]{0,1:T(8,128)(2,1)} %get-tuple-element.26) | data formatting | bytes 8388608 | tf_op jit(solution)/shard_map/add | solution.py:458
  113.2 6.4 %copy.22.refs_0_ = bf16[2048,1024]{1,0:T(8,128)(2,1)} copy(bf16[2048,1024]{0,1:T(8,128)(2,1)} %fusion.3) | data formatting | bytes 8388608 | tf_op jit(solution)/shard_map/convert_element_type | solution.py:23
  119.6 459.8 %backward_and_update.1 = (bf16[2,2,1024,3200]{3,2,1,0:T(8,128)(2,1)}, bf16[2,3200,1024]{2,1,0:T(8,128)(2,1)}, bf16[2,2,128,3200]{3,2,1,0:T(8,128)(2,1)}, bf16[2,...) custom-call(bf16[2048,1024]{1,0:T(8,128)(2,1)} %copy.22.refs_0_, bf16[1024,2048]{1,0:T(8,128)(2,1)} %fusion.34.refs_1_, ...), custom_call_target="tpu_custom_call" | custom-call | tf_op jit(solution)/shard_map/backward_and_update/pallas_call | solution.py:436
  579.3 0.0 copy-start.2
  579.4 0.0 copy-start.3
  579.4 19.7 %slice_bitcast_fusion = (bf16[2,1024,3200]{2,1,0:T(8,128)(2,1)}, bf16[2,1024,3200]{2,1,0:T(8,128)(2,1)}) fusion(bf16[2,2,1024,3200]{3,2,1,0:T(8,128)(2,1)} %get-tuple-element.13), kind=kLoop, calls=%fused_computation.1 | loop fusion | bytes 52428800 | tf_op jit(solution)/shard_map/squeeze | solution.py:464
  599.0 0.0 copy-done.3
  599.1 0.0 copy-start.4
  599.1 0.0 copy-start.5
  599.1 0.0 copy-start.6
  599.1 0.0 copy-start.7
  599.1 5.0 fusion.20
  604.1 1.2 copy-done.6
  605.3 0.9 copy-done.7
  606.2 8.2 %fusion.22 = (f32[2,128,3200]{2,1,0:T(8,128)}, f32[2,128,3200]{2,1,0:T(8,128)}, f32[2,128,3200]{2,1,0:T(8,128)}, f32[2,128,3200]{2,1,0:T(8,128)}) fusion(f32[2,128,3200]{2,1,0:T(8,128)S(1)} %copy-done.6, f32[2,128,3200]{2,1,0:T(8,128)S(1)} %copy-done.4, bf16[2,2,128,3200]{3,2,1,0:T(8,128)(2,1)} %get-tuple-element.15, f32[2,128,3200]{2,1,0:T(8,128)S(1)} %copy-done.5, ...), kind=kLoop, calls=%fused_computation.33 | loop fusion | flops 13107200 | bytes 29491200 | tf_op jit(solution)/shard_map/add | solution.py:27
  614.4 0.0 slice-done
  614.4 0.6 slice-done.2
  615.0 0.4 slice-done.3
  615.4 4.9 copy.31
  (15 shorter events, 0.0 us)
Async XLA Ops:
  7.1 3.4 copy-start
  97.8 5.7 copy-start.1
  579.3 19.7 %copy-start.2 = (f32[2,400,1024]{2,1,0:T(8,128)S(1)}, f32[2,400,1024]{2,1,0:T(8,128)}, u32[]{:S(2)}) copy-start(f32[2,400,1024]{2,1,0:T(8,128)} %refs_12_.1) | copy-start | bytes 9830404
  579.4 19.7 %copy-start.3 = (f32[2,400,1024]{2,1,0:T(8,128)S(1)}, f32[2,400,1024]{2,1,0:T(8,128)}, u32[]{:S(2)}) copy-start(f32[2,400,1024]{2,1,0:T(8,128)} %refs_15_.1) | copy-start | bytes 9830404
  579.4 19.7 %copy-start.8 = (bf16[2,400,1024]{2,1,0:T(8,128)(2,1)S(1)}, bf16[2,400,1024]{2,1,0:T(8,128)(2,1)}, u32[]{:S(2)}) copy-start(bf16[2,400,1024]{2,1,0:T(8,128)(2,1)} %get-tuple-element.16) | copy-start | bytes 4915204
  599.1 5.1 copy-start.4
  599.1 5.0 copy-start.5
  599.1 6.2 %copy-start.6 = (f32[2,128,3200]{2,1,0:T(8,128)S(1)}, f32[2,128,3200]{2,1,0:T(8,128)}, u32[]{:S(2)}) copy-start(f32[2,128,3200]{2,1,0:T(8,128)} %refs_13_.1) | copy-start | bytes 9830404
  599.1 7.1 %copy-start.7 = (f32[2,128,3200]{2,1,0:T(8,128)S(1)}, f32[2,128,3200]{2,1,0:T(8,128)}, u32[]{:S(2)}) copy-start(f32[2,128,3200]{2,1,0:T(8,128)} %refs_14_.1) | copy-start | bytes 9830404
  604.1 10.3 %slice-start = ((s8[13107200]{0:T(1024)(128)(4,1)}), s8[4194304]{0:T(1024)(128)(4,1)S(1)}, s32[]{:S(2)}) async-start(s8[13107200]{0:T(1024)(128)(4,1)} %bitcast.68), calls=%async_computation | async-start | bytes 8388608
  606.2 8.2 %slice-start.1 = ((s8[13107200]{0:T(1024)(128)(4,1)}), s8[4194304]{0:T(1024)(128)(4,1)S(1)}, s32[]{:S(2)}) async-start(s8[13107200]{0:T(1024)(128)(4,1)} %bitcast.68), calls=%async_computation.1 | async-start | bytes 8388608
  606.2 8.8 %slice-start.2 = ((s8[13107200]{0:T(1024)(128)(4,1)}), s8[4194304]{0:T(1024)(128)(4,1)S(1)}, s32[]{:S(2)}) async-start(s8[13107200]{0:T(1024)(128)(4,1)} %bitcast.68), calls=%async_computation.2 | async-start | bytes 8388608
  606.2 9.2 %slice-start.3 = ((s8[13107200]{0:T(1024)(128)(4,1)}), s8[524288]{0:T(1024)(128)(4,1)S(1)}, s32[]{:S(2)}) async-start(s8[13107200]{0:T(1024)(128)(4,1)} %bitcast.68), calls=%async_computation.3 | async-start | bytes 1048576

commit v2 on v1

v2 whole, which is shorter than its diff:
```python
import functools

import jax
import jax.numpy as jnp
from jax import lax
from jax.experimental import pallas as pl
from jax.experimental.pallas import tpu as pltpu
from jax.sharding import PartitionSpec as P

F32, BF16 = jnp.float32, jnp.bfloat16
PIECES = 5
TILE, SMALL = 512, 256
MESH = pl.DeviceIdType.MESH


def dot(a, b, ca=1, cb=0):
    return lax.dot_general(a, b, (((ca,), (cb,)), ((), ())), preferred_element_type=F32)


def norm(h):
    wide = h.astype(F32)
    scale = lax.rsqrt(jnp.mean(wide * wide, -1, keepdims=True) + 1e-6)
    return (wide * scale).astype(BF16)


def new_moments(m, v, g):
    return 0.9 * m + 0.1 * g, 0.95 * v + 0.05 * g * g


class Kind:
    pass


def wide_sum(*parts):
    total = parts[0].astype(F32)
    for part in parts[1:]:
        total = total + part.astype(F32)
    return total


def kernel(dims, *refs):
    T, D, FF, C, R, RB, PB = dims
    it = iter(refs)
    take = lambda n: [next(it) for _ in range(n)]
    x, dy = take(2)
    wg, wu, wd, mg, mu, md, vg, vu, vd = take(9)
    nw_g, nw_u, nw_d, g_a, g_b, dwd, h1, kept = take(8)
    a, at, d, dt, da, wgu, wdc, act, dgu, dwdc, grad = take(11)
    load_sem, w_sem, dwd_sem, tile_sem = take(4)
    kinds = []
    for name in "ab":
        k = Kind()
        k.name = name
        k.dd, k.s1, k.r1, k.s2, k.r2, k.m, k.v, k.w, k.nw, k.g = take(10)
        k.dd_s, k.dd_r, k.s1_s, k.s1_r, k.s2_s, k.s2_r = take(6)
        k.ax_s, k.ax_r, k.ah_s, k.ah_r, k.ad_s, k.ad_r, k.st_sem, k.out_sem, k.free = take(9)
        kinds.append(k)
    ka, kb = kinds
    kb.own, kb.own_sem = take(2)
    assert next(it, None) is None

    me = lax.axis_index("dp")
    chip, core = lax.div(me, 2), lax.rem(me, 2)
    other = 1 - core
    right, left, across = lax.rem(chip + 1, 4), lax.rem(chip + 3, 4), lax.rem(chip + 2, 4)
    partner = chip * 2 + other
    to = (right * 2 + core, left * 2 + core)
    frm = (left, right)

    barrier = pltpu.get_barrier_semaphore()
    for peer in (partner, *to):
        pl.semaphore_signal(barrier, inc=1, device_id={"dp": peer}, device_id_type=MESH)

    def remote(src, dst, send, recv, peer):
        return pltpu.make_async_remote_copy(src_ref=src, dst_ref=dst, send_sem=send, recv_sem=recv,
                                            device_id={"dp": peer}, device_id_type=MESH)

    local = pltpu.make_async_copy
    aligned = lambda i, n: pl.ds(pl.multiple_of(i * n, n), n)

    ka.na, ka.r, ka.n, ka.half = 2, R, C, (2, R // 2, C)
    kb.na, kb.r, kb.n, kb.half = 1, PB, D, (1, PB, D // 2)
    ka.first, ka.gap = 0, 2 * PIECES
    kb.first, kb.gap = PIECES, 2 * PIECES

    class Job:
        def __init__(self, k, since):
            late = lax.div(since, k.gap)
            self.layer, self.piece = 1 - late, since - late * k.gap
            self.turn = self.piece + late * PIECES
            self.slot, self.mark = lax.rem(self.turn, 2), lax.rem(self.turn, 8)

    def own_a(s, y):
        return grad.at[s.slot, :, y, core]

    ka.tile = own_a
    kb.tile = lambda s, y: kb.own.at[s.slot, :, y]

    def rows_b(j, p):
        return pl.ds(pl.multiple_of(j * RB + p * PB, PB), PB)

    def out_a(s, j, h=None):
        layer, c = s.layer, s.piece
        rows = aligned(j, R) if h is None else pl.ds(pl.multiple_of(j * R + h * (R // 2), R // 2), R // 2)
        return [nw.at[layer, rows, aligned(c, C)] for nw in (nw_g, nw_u)]

    def out_b(s, j, h=None):
        layer, p = s.layer, s.piece
        one = pl.ds(layer, 1)
        return [nw_d.at[one, rows_b(j, p)] if h is None else nw_d.at[one, rows_b(j, p), pl.ds(h * (D // 2), D // 2)]]

    ka.out, kb.out = out_a, out_b
    ka.mine = lambda s: [ka.nw.at[s.slot, i] for i in range(2)]
    kb.mine = lambda s: [kb.nw.at[s.slot]]
    ka.half_of = lambda ref, h: ref.at[:, pl.ds(h * (R // 2), R // 2), :]
    kb.half_of = lambda ref, h: ref.at[:, :, pl.ds(h * (D // 2), D // 2)]

    def state_copies(k, s):
        layer, c = s.layer, s.piece
        if k is ka:
            cols = aligned(c, C)
            out = []
            for i, (w, m, v) in enumerate(((wg, mg, vg), (wu, mu, vu))):
                out += [local(w.at[layer, aligned(me, R), cols], k.w.at[i], k.st_sem.at[3 * i]),
                        local(m.at[layer, :, cols], k.m.at[i], k.st_sem.at[3 * i + 1]),
                        local(v.at[layer, :, cols], k.v.at[i], k.st_sem.at[3 * i + 2])]
            return out
        rows = aligned(c, PB)
        one = pl.ds(layer, 1)
        return [local(wd.at[one, rows_b(me, c)], k.w, k.st_sem.at[0]),
                local(md.at[one, rows], k.m, k.st_sem.at[1]), local(vd.at[one, rows], k.v, k.st_sem.at[2])]

    def g_out(k, s):
        layer, c = s.layer, s.piece
        return g_a.at[layer, :, :, aligned(c, C)] if k is ka else g_b.at[pl.ds(layer, 1), aligned(c, PB)]

    def own_copies(k, s):
        slot = s.slot
        return [local(src, dst, k.out_sem.at[slot, 0]) for src, dst in zip(k.mine(s), k.out(s, me), strict=True)] + [
            local(k.g.at[slot], g_out(k, s), k.out_sem.at[slot, 1])]

    def own_wait(k, s):
        slot = s.slot
        local(k.nw.at[slot], k.nw.at[slot], k.out_sem.at[slot, 0]).wait()
        local(k.g.at[slot], k.g.at[slot], k.out_sem.at[slot, 1]).wait()

    def dd_copy(k, s):
        return remote(grad.at[s.slot, :, :, other], k.dd.at[s.slot], k.dd_s.at[s.slot], k.dd_r.at[s.slot], partner)

    def s1_copy(k, s, h):
        return remote(k.half_of(k.s1.at[s.slot], h), k.r1.at[s.slot, h], k.s1_s.at[s.slot, h], k.s1_r.at[s.slot, h], to[h])

    def s2_copy(k, s, h):
        return remote(k.s2.at[s.slot, h], k.r2.at[s.slot, h], k.s2_s.at[s.slot, h], k.s2_r.at[s.slot, h], to[h])

    def whole(k, send, recv, peer):
        return remote(k.nw.at[0], k.nw.at[0], send, recv, peer)

    def half(k, h, send, recv, peer):
        return remote(k.half_of(k.nw.at[0], h), k.half_of(k.nw.at[0], h), send, recv, peer)

    def ax_start(k, s, h):
        for src, dst in zip(k.mine(s), k.out(s, me), strict=True):
            remote(src, dst, k.ax_s.at[s.mark, h], k.ax_r.at[s.mark, h], to[h]).start()

    def ax_wait(k, s, h):
        return whole(k, k.ax_s.at[s.mark, h], k.ax_r.at[s.mark, h], to[h])

    def ah_start(k, s, h):
        for src in k.out(s, frm[h] * 2 + core, h):
            remote(src, src, k.ah_s.at[s.mark, h], k.ah_r.at[s.mark, h], to[h]).start()

    def ah_wait(k, s, h):
        return half(k, h, k.ah_s.at[s.mark, h], k.ah_r.at[s.mark, h], to[h])

    def ad_start(k, s, i):
        dst = k.out(s, (chip, left, right, across)[i] * 2 + core)
        for src, dst in zip(k.mine(s) if i == 0 else dst, dst, strict=True):
            remote(src, dst, k.ad_s.at[s.mark, i], k.ad_r.at[s.mark, i], partner).start()

    def ad_wait(k, s, i):
        return whole(k, k.ad_s.at[s.mark, i], k.ad_r.at[s.mark, i], partner)

    def blocks(k, body):
        rows, cols = k.half[1], k.half[2]
        for h in range(2):
            @pl.loop(0, rows // 16)
            def _(i):
                if k is ka:
                    cut = lambda ref: ref.at[:, pl.ds(pl.multiple_of(h * rows + i * 16, 16), 16), :]
                else:
                    cut = lambda ref: ref.at[:, pl.ds(pl.multiple_of(i * 16, 16), 16), pl.ds(h * cols, cols)]
                cut_half = lambda ref: ref.at[:, pl.ds(pl.multiple_of(i * 16, 16), 16), :]
                body(cut, cut_half, h)

    def stage_a(k, s):
        @pl.when(s.turn >= 2)
        def _():
            pl.semaphore_wait(k.free, 1)

        if k is ka:
            dd_copy(k, s).start()
            return
        layer, p = s.layer, s.piece
        for y in range(4):
            local(dwd.at[layer, pl.ds((y * 2 + core) * PIECES + p, 1)], k.own.at[s.slot, :, y], k.own_sem.at[s.slot]).start()
            remote(dwd.at[layer, pl.ds((y * 2 + other) * PIECES + p, 1)], k.dd.at[s.slot, :, y],
                   k.dd_s.at[s.slot], k.dd_r.at[s.slot], partner).start()

    def dd_wait(k, s):
        return remote(k.dd.at[s.slot], k.dd.at[s.slot], k.dd_s.at[s.slot], k.dd_r.at[s.slot], partner)

    def stage_b(k, s):
        slot = s.slot
        dd_wait(k, s).wait_recv()
        if k is kb:
            local(k.own.at[slot], k.own.at[slot], k.own_sem.at[slot]).wait()
        mine, theirs = k.tile(s, across), k.dd.at[slot, :, across]

        def body(cut, cut_half, h):
            cut(k.s1.at[slot])[...] = wide_sum(cut(mine)[...], cut(theirs)[...]).astype(BF16)

        blocks(k, body)
        for h in range(2):
            s1_copy(k, s, h).start()

    def stage_c(k, s):
        slot = s.slot
        for c in state_copies(k, s):
            c.start()
        for h in range(2):
            s1_copy(k, s, h).wait_recv()
        for way in range(2):
            y = (right, left)[way]
            mine, theirs = k.tile(s, y), k.dd.at[slot, :, y]

            def body(cut, cut_half, h):
                parts = [cut(mine)[...], cut(theirs)[...]]
                if h == way:
                    parts.append(cut_half(k.r1.at[slot, way])[...])
                cut(k.s2.at[slot, way])[...] = wide_sum(*parts).astype(BF16)

            blocks(k, body)
            s2_copy(k, s, way).start()
        for h in range(2):
            s1_copy(k, s, h).wait_send()
        dd_wait(k, s).wait_send()

    def stage_d(k, s):
        slot = s.slot
        for c in state_copies(k, s):
            c.wait()
        for h in range(2):
            s2_copy(k, s, h).wait_recv()
        mine, theirs = k.tile(s, chip), k.dd.at[slot, :, chip]

        def body(cut, cut_half, h):
            g = wide_sum(cut(mine)[...], cut(theirs)[...], cut(k.r2.at[slot, 0])[...], cut(k.r2.at[slot, 1])[...]).astype(BF16)
            cut(k.g.at[slot])[...] = g
            m, v = new_moments(cut(k.m)[...], cut(k.v)[...], g.astype(F32))
            w = cut(k.w)[...].astype(F32)
            cut(k.nw.at[slot])[...] = (w - 0.02 * (m * lax.rsqrt(v + 1e-8) + 0.1 * w)).astype(BF16)

        blocks(k, body)

        @pl.when(s.turn < 2 * PIECES - 2)
        def _():
            pl.semaphore_signal(k.free, inc=1, device_id={"dp": partner}, device_id_type=MESH)

        for h in range(2):
            ax_start(k, s, h)
        ad_start(k, s, 0)
        for c in own_copies(k, s):
            c.start()
        for h in range(2):
            s2_copy(k, s, h).wait_send()

    def stage_e(k, s):
        for h in range(2):
            ax_wait(k, s, h).wait_recv()
            ah_start(k, s, h)
            ad_start(k, s, 1 + h)
        ad_wait(k, s, 0).wait_recv()
        own_wait(k, s)
        for h in range(2):
            ax_wait(k, s, h).wait_send()
        ad_wait(k, s, 0).wait_send()

    def stage_f(k, s):
        for h in range(2):
            ah_wait(k, s, h).wait_recv()
        ad_start(k, s, 3)

    def stage_g(k, s):
        for i in range(1, 4):
            ad_wait(k, s, i).wait_recv()
        for h in range(2):
            ah_wait(k, s, h).wait_send()
        for i in range(1, 4):
            ad_wait(k, s, i).wait_send()

    def run(stage, k, s):
        since = s - k.first

        @pl.when((since >= 0) & (since < 2 * k.gap) & (lax.rem(since, k.gap) < PIECES))
        def _():
            stage(k, Job(k, since))

    def before(s):
        for stage, lag in ((stage_e, 3), (stage_d, 2), (stage_c, 1)):
            for k in kinds:
                run(stage, k, s - lag)

    def send(s):
        for k in kinds:
            run(stage_a, k, s)

    def after(s):
        for stage, lag in ((stage_f, 4), (stage_b, 0), (stage_g, 5)):
            for k in kinds:
                run(stage, k, s - lag)

    def up_copies(layer, c):
        cols = aligned(c, C)
        return (local(wg.at[layer, :, cols], wgu.at[lax.rem(c, 2), :, pl.ds(0, C)], w_sem.at[lax.rem(c, 2), 0]),
                local(wu.at[layer, :, cols], wgu.at[lax.rem(c, 2), :, pl.ds(C, C)], w_sem.at[lax.rem(c, 2), 1]))

    def down_copy(layer, c):
        return local(wd.at[layer, aligned(c, C)], wdc, w_sem.at[0, 2])

    def start(copies):
        for copy in copies:
            copy.start()

    def wait(copies):
        for copy in copies:
            copy.wait()

    def next_up(layer, c):
        @pl.when(c < PIECES - 1)
        def _():
            start(up_copies(layer, c + 1))

    def put(ref, c, rows, value):
        @pl.when(c == 0)
        def _():
            ref[rows, :] = value

        @pl.when(c > 0)
        def _():
            ref[rows, :] += value

    def dwd_copy(layer, c):
        return local(dwdc, dwd.at[layer, pl.ds(c * 8, 8)], dwd_sem)

    def dgu_copy(c, rows, back, sem):
        there = kept.at[c, rows]
        return local(there, dgu.at[rows], sem) if back else local(dgu.at[rows], there, sem)

    every = pl.ds(0, T)
    wide_rows = lambda ref: ref.at[:, pl.ds(0, D)]

    def chunks(layer):
        first = (1 - layer) * 2 * PIECES

        @pl.loop(0, PIECES)
        def _(c):
            s = c + first
            wait(up_copies(layer, c))
            next_up(layer, c)
            down_copy(layer, c).wait()
            if layer:
                @pl.when(c > 0)
                def _():
                    dgu_copy(c, every, False, load_sem.at[2]).wait()

            def tokens(i):
                rows = aligned(i, SMALL)
                gu = dot(a[rows, :], wgu[lax.rem(c, 2)])
                dact = dot(d[rows, :], wdc[...], 1, 1).astype(BF16).astype(F32)
                gate, up = gu[:, :C], gu[:, C:]
                sig = jax.nn.sigmoid(gate)
                silu = gate * sig
                act[rows, :] = (silu * up).astype(BF16)
                dgu[rows, :C] = (dact * up * (sig * (1 + gate * (1 - sig)))).astype(BF16)
                dgu[rows, C:] = (dact * silu).astype(BF16)

            pl.loop(0, T // SMALL // 2)(tokens)
            before(s)
            pl.loop(T // SMALL // 2, T // SMALL)(tokens)
            if layer:
                dgu_copy(c, every, False, load_sem.at[2]).start()

            @pl.when(c < PIECES - 1)
            def _():
                down_copy(layer, c + 1).start()

            @pl.loop(0, 2)
            def _(j):
                block = dot(at[aligned(j, D // 2), :], dgu[...]).astype(BF16)
                for i in range(2):
                    grad[lax.rem(c + (1 - layer) * PIECES, 2), i, pl.ds(j * 2, 2)] = block[:, i * C : (i + 1) * C].reshape(2, 2, R, C)

            send(s)

            @pl.when(c > 0)
            def _():
                dwd_copy(layer, c - 1).wait()

            for j in range(4):
                block = dot(dt[j * (D // 4) : (j + 1) * (D // 4), :], act[...]).astype(BF16)
                dwdc[:, :, j * (D // 4) : (j + 1) * (D // 4)] = block.T.reshape(8, PB, D // 4)
            dwd_copy(layer, c).start()
            after(s)

        dwd_copy(layer, PIECES - 1).wait()

    bring = [local(x, a, load_sem.at[0]), local(dy, d, load_sem.at[1]), local(x, wide_rows(dgu), load_sem.at[2])]
    start(bring)
    start(up_copies(0, 0))
    down_copy(0, 0).start()
    wait(bring[:1])

    @pl.loop(0, T // 128)
    def _(i):
        rows = aligned(i, 128)
        a[rows, :] = norm(a[rows, :])

    @pl.loop(0, PIECES)
    def _(c):
        wait(up_copies(0, c))
        next_up(0, c)
        down_copy(0, c).wait()

        @pl.loop(0, T // TILE)
        def _(i):
            rows = aligned(i, TILE)
            gu = dot(a[rows, :], wgu[lax.rem(c, 2)])
            gate = gu[:, :C]
            act[rows, :] = (gate * jax.nn.sigmoid(gate) * gu[:, C:]).astype(BF16)
            put(da, c, rows, dot(act[rows, :], wdc[...]))

        @pl.when(c < PIECES - 1)
        def _():
            down_copy(0, c + 1).start()

    start(up_copies(1, 0))
    down_copy(1, 0).start()
    wait(bring[1:])

    @pl.loop(0, T // 128)
    def _(i):
        rows = aligned(i, 128)
        h = dgu[rows, :D] + da[rows, :].astype(BF16)
        dgu[rows, :D] = h
        low = norm(h)
        a[rows, :] = low
        at[:, rows] = low.T
        dt[:, rows] = d[rows, :].T

    keep = local(wide_rows(dgu), h1, load_sem.at[0])
    keep.start()
    pl.semaphore_wait(barrier, 3)
    keep.wait()

    chunks(1)

    bring = local(h1, a, load_sem.at[0])
    bring.start()
    start(up_copies(1, 0))
    dgu_copy(PIECES - 1, every, False, load_sem.at[2]).wait()
    tiles = T // TILE

    @pl.loop(0, tiles)
    def _(i):
        dgu_copy(0, aligned(i, TILE), True, tile_sem.at[i]).start()

    @pl.loop(0, PIECES)
    def _(c):
        s = c + PIECES
        wait(up_copies(1, c))
        next_up(1, c)

        def tokens(i):
            rows = aligned(i, TILE)
            dgu_copy(c, rows, True, tile_sem.at[i]).wait()
            put(da, c, rows, dot(dgu[rows, :], wgu[lax.rem(c, 2)], 1, 1))

            @pl.when(c < PIECES - 1)
            def _():
                dgu_copy(c + 1, rows, True, tile_sem.at[i]).start()

        before(s)
        send(s)
        pl.loop(0, tiles)(tokens)
        after(s)

    again = local(x, wide_rows(dgu), load_sem.at[1])
    again.start()
    start(up_copies(0, 0))
    down_copy(0, 0).start()
    bring.wait()

    @pl.loop(0, T // 128)
    def _(i):
        rows = aligned(i, 128)
        wide = a[rows, :].astype(F32)
        scale = lax.rsqrt(jnp.mean(wide * wide, -1, keepdims=True) + 1e-6)
        by = da[rows, :].astype(BF16).astype(F32)
        inner = jnp.mean(wide * by, -1, keepdims=True)
        total = d[rows, :] + (by * scale - wide * (inner * scale * scale * scale)).astype(BF16)
        d[rows, :] = total
        dt[:, rows] = total.T

    again.wait()

    @pl.loop(0, T // 128)
    def _(i):
        rows = aligned(i, 128)
        low = norm(dgu[rows, :D])
        a[rows, :] = low
        at[:, rows] = low.T

    chunks(0)

    @pl.loop(3 * PIECES, 4 * PIECES + 5)
    def _(s):
        before(s)
        send(s)
        after(s)


def gathered_step(mesh, dims, operands):
    T, D, FF, C, R, RB, PB = dims
    hbm = pl.BlockSpec(memory_space=pl.ANY)
    vmem, dma = pltpu.VMEM, pltpu.SemaphoreType.DMA
    shapes = [vmem((T, D), BF16), vmem((D, T), BF16), vmem((T, D), BF16), vmem((D, T), BF16), vmem((T, D), F32)]
    shapes += [vmem((2, D, 2 * C), BF16), vmem((C, D), BF16), vmem((T, C), BF16), vmem((T, 2 * C), BF16)]
    shapes += [vmem((8, PB, D), BF16), vmem((2, 2, 4, 2, R, C), BF16)]
    shapes += [dma((3,)), dma((2, 3)), dma, dma((T // TILE,))]
    for na, r, n, half in ((2, R, C, (2, R // 2, C)), (1, PB, D, (1, PB, D // 2))):
        tile = (na, r, n)
        shapes += [vmem((2, na, 4, r, n), BF16), vmem((2, *tile), BF16), vmem((2, 2, *half), BF16), vmem((2, 2, *tile), BF16),
                   vmem((2, 2, *tile), BF16), vmem(tile, F32), vmem(tile, F32), vmem(tile, BF16), vmem((2, *tile), BF16),
                   vmem((2, *tile), BF16)]
        shapes += [dma((2,)), dma((2,)), dma((2, 2)), dma((2, 2)), dma((2, 2)), dma((2, 2))]
        shapes += [dma((8, 2)), dma((8, 2)), dma((8, 2)), dma((8, 2)), dma((8, 4)), dma((8, 4)), dma((6,)), dma((2, 2)),
                   pltpu.SemaphoreType.REGULAR]
    shapes += [vmem((2, 1, 4, PB, D), BF16), dma((2,))]
    out = lambda *s: jax.ShapeDtypeStruct(s, BF16)
    L = 2
    return pl.pallas_call(
        functools.partial(kernel, dims),
        out_shape=(out(L, D, FF), out(L, D, FF), out(L, FF, D), out(L, 2, R, FF), out(L, RB, D), out(L, 8 * PIECES, PB, D),
                   out(T, D), out(PIECES, T, 2 * C)),
        in_specs=[hbm] * len(operands),
        out_specs=(hbm,) * 8,
        scratch_shapes=shapes,
        compiler_params=pltpu.CompilerParams(collective_id=0, has_side_effects=True, vmem_limit_bytes=67_000_000),
        name="step",
    )(*operands)


def solution(mesh):
    assert mesh.shape["dp"] == 8

    def body(x, dy, wg, wu, wd, mg, mu, md, vg, vu, vd):
        T, D = x.shape[1:]
        FF = wg.shape[2]
        dims = (T, D, FF, FF // PIECES, D // 8, FF // 8, FF // 8 // PIECES)
        nw_g, nw_u, nw_d, g_a, g_b, *_ = gathered_step(mesh, dims, (x[0], dy[0], wg, wu, wd, mg, mu, md, vg, vu, vd))
        g = [g_a[:, 0], g_a[:, 1], g_b]
        new = [new_moments(m, v, t.astype(F32)) for m, v, t in zip((mg, mu, md), (vg, vu, vd), g, strict=True)]
        return (nw_g, nw_u, nw_d, *(t[0] for t in new), *(t[1] for t in new))

    seq, rep, rows = P(("rep", "dp")), P(), P(None, "dp")
    return jax.shard_map(
        body, mesh=mesh, in_specs=(seq, seq, rep, rep, rep) + (rows,) * 6,
        out_specs=(P("rep"),) * 3 + (P("rep", "dp"),) * 6, check_vma=False)
```

time: 630 us -> 525 us (0.83); the launches traced: 621 us -> 525 us
  matrix products: 67.9 us -> 0 us
  local copies, waits for them, and re-layouts: 60.1 us -> 22.7 us
  Pallas kernels: 460 us -> 484 us
  other arithmetic: 31.8 us -> 18.1 us
    dot_general x3 -> x0, matrix products: 67.9 us -> none  [dot(): lax.dot_general(a, b, (((ca,), (cb,)), ((), ())), preferred_element_type=...]
    pallas_call x1, Pallas kernels: 460 us -> 484 us  [gathered_step(): pl.pallas_call(functools.partial(kernel, dims), out_shape=(out(L, D, FF),...]
    squeeze x1 -> x0, local copies, waits for them, and re-layouts: 19.7 us -> none  [body(): nw_a[:, 1]]
    convert_element_type x2 -> x0, local copies, waits for them, and re-layouts: 12.8 us -> none  [norm(): return (wide * scale).astype(BF16)]
    transpose x2 -> x0, other arithmetic: 9 us -> none  [body(): operands = (a1, a1.T, dy, dy.T, h1, a0, a0.T, wg, wu, wd, mg, mu, md, vg,...]
    add x1 -> x0, local copies, waits for them, and re-layouts: 6.42 us -> none  [body(): h1 = x + dot((jax.nn.silu(gate) * up).astype(BF16), wd[0]).astype(BF16)]
    convert_element_type x2 -> x0, other arithmetic: 6.4 us -> none  [norm(): return (wide * scale).astype(BF16)]
where the time goes in v2:
time: 525 us
  Pallas kernels  484 us (92%)
  local copies, waits for them, and re-layouts  22.7 us (4%)
  other arithmetic  18.1 us (3%)
    pallas_call x1, Pallas kernels, gathered_step(): pl.pallas_call(functools.partial(kernel, dims), out_shape=(out(L, D, FF),...  484 us
    unnamed x29, local copies, waits for them, and re-layouts  22.7 us
    add x2, other arithmetic, new_moments(): return (0.9 * m + 0.1 * g, 0.95 * v + 0.05 * g * g)  18.1 us

profile of v2, /device:TPU:113, one launch (start us, length us, event | category | flops | bytes accessed | tf_op | source)
XLA Modules:
  0.0 525.1 jit_solution(17172674314207547916)
XLA Ops:
  0.6 483.6 %step.1 = (bf16[2,1024,3200]{2,1,0:T(8,128)(2,1)}, bf16[2,1024,3200]{2,1,0:T(8,128)(2,1)}, bf16[2,3200,1024]{2,1,0:T(8,128)(2,1)}, bf16[2,2,128,3200]{3,2,1,0:T(...) custom-call(bf16[2048,1024]{1,0:T(8,128)(2,1)} %bitcast.19, ...), custom_call_target="tpu_custom_call" | custom-call | tf_op jit(solution)/shard_map/step/pallas_call | solution.py:552
  484.3 0.0 copy-start
  484.3 0.0 slice-start.8
  484.3 0.0 slice-start.9
  484.3 8.0 %fusion.1 = (f32[2,400,1024]{2,1,0:T(8,128)}, f32[2,400,1024]{2,1,0:T(8,128)}) fusion(bf16[2,400,1024]{2,1,0:T(8,128)(2,1)} %get-tuple-element.18, f32[2,400,1024]{2,1,0:T(8,128)} %refs_10_.1, f32[2,400,1024]{2,1,0:T(8,128)} %refs_7_.1), kind=kLoop, calls=%fused_computation.9 | loop fusion | flops 6553600 | bytes 14745600 | tf_op jit(solution)/shard_map/add | solution.py:27
  492.3 0.0 copy-done
  492.3 0.0 slice-start.10
  492.3 0.0 slice-start.11
  492.3 0.0 slice-start.4
  492.3 0.0 slice-start.5
  492.3 0.0 slice-start.6
  492.4 10.0 %fusion.3 = (f32[2,128,3200]{2,1,0:T(8,128)}, f32[2,128,3200]{2,1,0:T(8,128)}, f32[2,128,3200]{2,1,0:T(8,128)}, f32[2,128,3200]{2,1,0:T(8,128)}) fusion(f32[2,128,3200]{2,1,0:T(8,128)} %refs_8_.1, f32[2,128,3200]{2,1,0:T(8,128)S(1)} %copy-done, bf16[2,2,128,3200]{3,2,1,0:T(8,128)(2,1)} %get-tuple-element.17, f32[2,128,3200]{2,1,0:T(8,128)} %refs_6_.1, ...), kind=kLoop, calls=%fused_computation.11 | loop fusion | flops 13107200 | bytes 29491200 | tf_op jit(solution)/shard_map/add | solution.py:27
  502.4 0.0 slice-done.8
  502.4 0.0 slice-done.9
  502.4 0.0 slice-done.10
  502.4 0.0 slice-done.11
  502.4 0.0 slice-start.7
  502.4 0.0 slice-start
  502.4 0.0 slice-start.1
  502.5 0.0 slice-start.2
  502.5 6.6 %copy.26 = bf16[2,1024,3200]{2,1,0:T(8,128)(2,1)} copy(bf16[2,1024,3200]{2,1,0:T(8,128)(2,1)S(1)} %bitcast.18) | data formatting | bytes 26214400
  509.1 0.0 slice-done.4
  509.1 1.1 slice-done.5
  510.2 0.0 slice-done.6
  510.3 1.4 slice-done.7
  511.6 0.0 slice-start.3
  511.6 6.6 %copy.27 = bf16[2,1024,3200]{2,1,0:T(8,128)(2,1)} copy(bf16[2,1024,3200]{2,1,0:T(8,128)(2,1)S(1)} %bitcast.16) | data formatting | bytes 26214400
  518.3 0.0 slice-done
  518.3 0.0 slice-done.1
  518.3 1.7 slice-done.2
  520.0 0.2 slice-done.3
  520.1 4.9 copy.28
  (3 shorter events, 0.0 us)
Async XLA Ops:
  484.3 8.1 %copy-start = (f32[2,128,3200]{2,1,0:T(8,128)S(1)}, f32[2,128,3200]{2,1,0:T(8,128)}, u32[]{:S(2)}) copy-start(f32[2,128,3200]{2,1,0:T(8,128)} %refs_5_.1) | copy-start | bytes 9830404
  484.3 18.1 %slice-start.8 = ((s8[13107200]{0:T(1024)(128)(4,1)}), s8[4194304]{0:T(1024)(128)(4,1)S(1)}, s32[]{:S(2)}) async-start(s8[13107200]{0:T(1024)(128)(4,1)} %bitcast.17), calls=%async_computation.8 | async-start | bytes 8388608
  484.3 18.1 %slice-start.9 = ((s8[13107200]{0:T(1024)(128)(4,1)}), s8[4194304]{0:T(1024)(128)(4,1)S(1)}, s32[]{:S(2)}) async-start(s8[13107200]{0:T(1024)(128)(4,1)} %bitcast.17), calls=%async_computation.9 | async-start | bytes 8388608
  492.3 10.1 %slice-start.10 = ((s8[13107200]{0:T(1024)(128)(4,1)}), s8[4194304]{0:T(1024)(128)(4,1)S(1)}, s32[]{:S(2)}) async-start(s8[13107200]{0:T(1024)(128)(4,1)} %bitcast.17), calls=%async_computation.10 | async-start | bytes 8388608
  492.3 10.1 %slice-start.11 = ((s8[13107200]{0:T(1024)(128)(4,1)}), s8[524288]{0:T(1024)(128)(4,1)S(1)}, s32[]{:S(2)}) async-start(s8[13107200]{0:T(1024)(128)(4,1)} %bitcast.17), calls=%async_computation.11 | async-start | bytes 1048576
  492.3 16.8 %slice-start.4 = ((s8[13107200]{0:T(1024)(128)(4,1)}), s8[4194304]{0:T(1024)(128)(4,1)S(1)}, s32[]{:S(2)}) async-start(s8[13107200]{0:T(1024)(128)(4,1)} %bitcast.15), calls=%async_computation.4 | async-start | bytes 8388608
  492.3 17.9 %slice-start.5 = ((s8[13107200]{0:T(1024)(128)(4,1)}), s8[4194304]{0:T(1024)(128)(4,1)S(1)}, s32[]{:S(2)}) async-start(s8[13107200]{0:T(1024)(128)(4,1)} %bitcast.15), calls=%async_computation.5 | async-start | bytes 8388608
  492.3 17.9 %slice-start.6 = ((s8[13107200]{0:T(1024)(128)(4,1)}), s8[524288]{0:T(1024)(128)(4,1)S(1)}, s32[]{:S(2)}) async-start(s8[13107200]{0:T(1024)(128)(4,1)} %bitcast.15), calls=%async_computation.6 | async-start | bytes 1048576
  502.4 9.2 %slice-start.7 = ((s8[13107200]{0:T(1024)(128)(4,1)}), s8[4194304]{0:T(1024)(128)(4,1)S(1)}, s32[]{:S(2)}) async-start(s8[13107200]{0:T(1024)(128)(4,1)} %bitcast.15), calls=%async_computation.7 | async-start | bytes 8388608
  502.4 15.9 %slice-start = ((s8[13107200]{0:T(1024)(128)(4,1)}), s8[4194304]{0:T(1024)(128)(4,1)S(1)}, s32[]{:S(2)}) async-start(s8[13107200]{0:T(1024)(128)(4,1)} %bitcast.13), calls=%async_computation | async-start | bytes 8388608
  502.4 15.8 %slice-start.1 = ((s8[13107200]{0:T(1024)(128)(4,1)}), s8[4194304]{0:T(1024)(128)(4,1)S(1)}, s32[]{:S(2)}) async-start(s8[13107200]{0:T(1024)(128)(4,1)} %bitcast.13), calls=%async_computation.1 | async-start | bytes 8388608
  502.5 17.5 %slice-start.2 = ((s8[13107200]{0:T(1024)(128)(4,1)}), s8[4194304]{0:T(1024)(128)(4,1)S(1)}, s32[]{:S(2)}) async-start(s8[13107200]{0:T(1024)(128)(4,1)} %bitcast.13), calls=%async_computation.2 | async-start | bytes 8388608
  511.6 8.5 %slice-start.3 = ((s8[13107200]{0:T(1024)(128)(4,1)}), s8[524288]{0:T(1024)(128)(4,1)S(1)}, s32[]{:S(2)}) async-start(s8[13107200]{0:T(1024)(128)(4,1)} %bitcast.13), calls=%async_computation.3 | async-start | bytes 1048576

commit v3 on v2

--- a/solution.py
+++ b/solution.py
@@ -385,15 +385,15 @@
                 dgu[rows, :C] = (dact * up * (sig * (1 + gate * (1 - sig)))).astype(BF16)
                 dgu[rows, C:] = (dact * silu).astype(BF16)
 
-            pl.loop(0, T // SMALL // 2)(tokens)
-            before(s)
-            pl.loop(T // SMALL // 2, T // SMALL)(tokens)
+            pl.loop(0, T // SMALL)(tokens)
             if layer:
                 dgu_copy(c, every, False, load_sem.at[2]).start()
 
             @pl.when(c < PIECES - 1)
             def _():
                 down_copy(layer, c + 1).start()
+
+            before(s)
 
             @pl.loop(0, 2)
             def _(j):
@@ -490,9 +490,10 @@
             def _():
                 dgu_copy(c + 1, rows, True, tile_sem.at[i]).start()
 
+        pl.loop(0, tiles // 2)(tokens)
         before(s)
         send(s)
-        pl.loop(0, tiles)(tokens)
+        pl.loop(tiles // 2, tiles)(tokens)
         after(s)
 
     again = local(x, wide_rows(dgu), load_sem.at[1])

time: 525 us -> 530 us (level)
  no operation moved by 1% of the time
where the time goes in v3:
time: 530 us; the launch traced here: 528 us
  Pallas kernels  487 us (92%)
  local copies, waits for them, and re-layouts  22.7 us (4%)
  other arithmetic  18.1 us (3%)
    pallas_call x1, Pallas kernels, gathered_step(): pl.pallas_call(functools.partial(kernel, dims), out_shape=(out(L, D, FF),...  487 us
    unnamed x29, local copies, waits for them, and re-layouts  22.7 us
    add x2, other arithmetic, new_moments(): return (0.9 * m + 0.1 * g, 0.95 * v + 0.05 * g * g)  18.1 us

profile of v3, /device:TPU:113, one launch (start us, length us, event | category | flops | bytes accessed | tf_op | source)
XLA Modules:
  0.0 528.5 jit_solution(13678004495068962951)
XLA Ops:
  0.6 487.0 %step.1 = (bf16[2,1024,3200]{2,1,0:T(8,128)(2,1)}, bf16[2,1024,3200]{2,1,0:T(8,128)(2,1)}, bf16[2,3200,1024]{2,1,0:T(8,128)(2,1)}, bf16[2,2,128,3200]{3,2,1,0:T(...) custom-call(bf16[2048,1024]{1,0:T(8,128)(2,1)} %bitcast.19, ...), custom_call_target="tpu_custom_call" | custom-call | tf_op jit(solution)/shard_map/step/pallas_call | solution.py:553
  487.6 0.0 copy-start
  487.7 0.0 slice-start.8
  487.7 0.0 slice-start.9
  487.7 8.0 %fusion.1 = (f32[2,400,1024]{2,1,0:T(8,128)}, f32[2,400,1024]{2,1,0:T(8,128)}) fusion(bf16[2,400,1024]{2,1,0:T(8,128)(2,1)} %get-tuple-element.18, f32[2,400,1024]{2,1,0:T(8,128)} %refs_10_.1, f32[2,400,1024]{2,1,0:T(8,128)} %refs_7_.1), kind=kLoop, calls=%fused_computation.9 | loop fusion | flops 6553600 | bytes 14745600 | tf_op jit(solution)/shard_map/add | solution.py:27
  495.7 0.0 copy-done
  495.7 0.0 slice-start.10
  495.7 0.0 slice-start.11
  495.7 0.0 slice-start.4
  495.7 0.0 slice-start.5
  495.7 0.0 slice-start.6
  495.7 10.0 %fusion.3 = (f32[2,128,3200]{2,1,0:T(8,128)}, f32[2,128,3200]{2,1,0:T(8,128)}, f32[2,128,3200]{2,1,0:T(8,128)}, f32[2,128,3200]{2,1,0:T(8,128)}) fusion(f32[2,128,3200]{2,1,0:T(8,128)} %refs_8_.1, f32[2,128,3200]{2,1,0:T(8,128)S(1)} %copy-done, bf16[2,2,128,3200]{3,2,1,0:T(8,128)(2,1)} %get-tuple-element.17, f32[2,128,3200]{2,1,0:T(8,128)} %refs_6_.1, ...), kind=kLoop, calls=%fused_computation.11 | loop fusion | flops 13107200 | bytes 29491200 | tf_op jit(solution)/shard_map/add | solution.py:27
  505.8 0.0 slice-done.8
  505.8 0.0 slice-done.9
  505.8 0.0 slice-done.10
  505.8 0.0 slice-done.11
  505.8 0.0 slice-start.7
  505.8 0.0 slice-start
  505.8 0.0 slice-start.1
  505.8 0.0 slice-start.2
  505.9 6.6 %copy.26 = bf16[2,1024,3200]{2,1,0:T(8,128)(2,1)} copy(bf16[2,1024,3200]{2,1,0:T(8,128)(2,1)S(1)} %bitcast.18) | data formatting | bytes 26214400
  512.5 0.0 slice-done.4
  512.5 1.1 slice-done.5
  513.6 0.0 slice-done.6
  513.7 1.4 slice-done.7
  515.0 0.0 slice-start.3
  515.0 6.6 %copy.27 = bf16[2,1024,3200]{2,1,0:T(8,128)(2,1)} copy(bf16[2,1024,3200]{2,1,0:T(8,128)(2,1)S(1)} %bitcast.16) | data formatting | bytes 26214400
  521.7 0.0 slice-done
  521.7 0.0 slice-done.1
  521.7 1.7 slice-done.2
  523.4 0.2 slice-done.3
  523.5 4.9 copy.28
  (3 shorter events, 0.0 us)
Async XLA Ops:
  487.6 8.1 %copy-start = (f32[2,128,3200]{2,1,0:T(8,128)S(1)}, f32[2,128,3200]{2,1,0:T(8,128)}, u32[]{:S(2)}) copy-start(f32[2,128,3200]{2,1,0:T(8,128)} %refs_5_.1) | copy-start | bytes 9830404
  487.7 18.1 %slice-start.8 = ((s8[13107200]{0:T(1024)(128)(4,1)}), s8[4194304]{0:T(1024)(128)(4,1)S(1)}, s32[]{:S(2)}) async-start(s8[13107200]{0:T(1024)(128)(4,1)} %bitcast.17), calls=%async_computation.8 | async-start | bytes 8388608
  487.7 18.1 %slice-start.9 = ((s8[13107200]{0:T(1024)(128)(4,1)}), s8[4194304]{0:T(1024)(128)(4,1)S(1)}, s32[]{:S(2)}) async-start(s8[13107200]{0:T(1024)(128)(4,1)} %bitcast.17), calls=%async_computation.9 | async-start | bytes 8388608
  495.7 10.1 %slice-start.10 = ((s8[13107200]{0:T(1024)(128)(4,1)}), s8[4194304]{0:T(1024)(128)(4,1)S(1)}, s32[]{:S(2)}) async-start(s8[13107200]{0:T(1024)(128)(4,1)} %bitcast.17), calls=%async_computation.10 | async-start | bytes 8388608
  495.7 10.1 %slice-start.11 = ((s8[13107200]{0:T(1024)(128)(4,1)}), s8[524288]{0:T(1024)(128)(4,1)S(1)}, s32[]{:S(2)}) async-start(s8[13107200]{0:T(1024)(128)(4,1)} %bitcast.17), calls=%async_computation.11 | async-start | bytes 1048576
  495.7 16.8 %slice-start.4 = ((s8[13107200]{0:T(1024)(128)(4,1)}), s8[4194304]{0:T(1024)(128)(4,1)S(1)}, s32[]{:S(2)}) async-start(s8[13107200]{0:T(1024)(128)(4,1)} %bitcast.15), calls=%async_computation.4 | async-start | bytes 8388608
  495.7 17.9 %slice-start.5 = ((s8[13107200]{0:T(1024)(128)(4,1)}), s8[4194304]{0:T(1024)(128)(4,1)S(1)}, s32[]{:S(2)}) async-start(s8[13107200]{0:T(1024)(128)(4,1)} %bitcast.15), calls=%async_computation.5 | async-start | bytes 8388608
  495.7 17.9 %slice-start.6 = ((s8[13107200]{0:T(1024)(128)(4,1)}), s8[524288]{0:T(1024)(128)(4,1)S(1)}, s32[]{:S(2)}) async-start(s8[13107200]{0:T(1024)(128)(4,1)} %bitcast.15), calls=%async_computation.6 | async-start | bytes 1048576
  505.8 9.2 %slice-start.7 = ((s8[13107200]{0:T(1024)(128)(4,1)}), s8[4194304]{0:T(1024)(128)(4,1)S(1)}, s32[]{:S(2)}) async-start(s8[13107200]{0:T(1024)(128)(4,1)} %bitcast.15), calls=%async_computation.7 | async-start | bytes 8388608
  505.8 15.9 %slice-start = ((s8[13107200]{0:T(1024)(128)(4,1)}), s8[4194304]{0:T(1024)(128)(4,1)S(1)}, s32[]{:S(2)}) async-start(s8[13107200]{0:T(1024)(128)(4,1)} %bitcast.13), calls=%async_computation | async-start | bytes 8388608
  505.8 15.8 %slice-start.1 = ((s8[13107200]{0:T(1024)(128)(4,1)}), s8[4194304]{0:T(1024)(128)(4,1)S(1)}, s32[]{:S(2)}) async-start(s8[13107200]{0:T(1024)(128)(4,1)} %bitcast.13), calls=%async_computation.1 | async-start | bytes 8388608
  505.8 17.5 %slice-start.2 = ((s8[13107200]{0:T(1024)(128)(4,1)}), s8[4194304]{0:T(1024)(128)(4,1)S(1)}, s32[]{:S(2)}) async-start(s8[13107200]{0:T(1024)(128)(4,1)} %bitcast.13), calls=%async_computation.2 | async-start | bytes 8388608
  515.0 8.5 %slice-start.3 = ((s8[13107200]{0:T(1024)(128)(4,1)}), s8[524288]{0:T(1024)(128)(4,1)S(1)}, s32[]{:S(2)}) async-start(s8[13107200]{0:T(1024)(128)(4,1)} %bitcast.13), calls=%async_computation.3 | async-start | bytes 1048576
